TPU v7x, 32 devices: a whole 2x2x4 slice. The times are simulated.
32 devices in a mesh: grp: 4 (over y, x), grid: 8 (over z, core).
Axes of the slice: x: 2, y: 2, z: 4, core: 2. Of those that a mesh axis runs over, the one named last changes fastest.
Arguments:
- orbitals: float32 [64, 262144], P('grp', 'grid'), may hold values from -6 to 6
- anchors: int32 [64, 3], replicated, may hold values from 0 to 31
- pair_slots: int32 [32, 4, 2], replicated, may hold values from -1 to 63, as said below
Outputs:
- exchange_term: float32 [64, 262144], P('grp', 'grid')
Inputs may be any that keep to these rules, and one draw needn't show every extreme that they name: `pair_slots`: row k lists the pairs of owner k, the device with index k in the order grp, grid; its first slots hold pairs of two different orbital numbers and its other slots hold -1 in both columns. Exactly 64 slots hold pairs in all, no row holds more than 4, and some row holds exactly 4.
All inputs are finite; a program needn't handle non-finite values.
Results may differ from a plain program's by a relative error of at most 0.0003.
Values sent between devices are 32-bit elements; how exact they have to be, the bound alone decides.
A program may use at most 128 MiB of HBM per device.

v0:
```python
import math

import jax
import jax.numpy as jnp
from jax import lax
from jax.experimental import pallas as pl
from jax.experimental.pallas import tpu as pltpu
from jax.sharding import PartitionSpec as P

B = 64
PAIR_DEV = 2
ITERS = 3
MOST_CHUNKS = 2
LANES = 128
ROWS = B * B // LANES
PAD = 32
STEP = 4


def deal_evenly(pair_slots, owner_count, each_owner):
    flat_slots = pair_slots.reshape(-1, 2)
    filled = (flat_slots[:, 0] >= 0).astype(jnp.int32)
    position = jnp.cumsum(filled, dtype=jnp.int32) - filled
    wanted = lax.broadcasted_iota(jnp.int32, (owner_count, each_owner), 1) * owner_count
    wanted = (wanted + lax.broadcasted_iota(jnp.int32, (owner_count, each_owner), 0)).reshape(-1)
    matched = (position[None, :] == wanted[:, None]) & (filled[None, :] == 1)
    picked = jnp.sum(jnp.where(matched[:, :, None], flat_slots[None], 0), axis=1)
    return picked.reshape(owner_count, each_owner, 2)


def gather_kernel(ids_ref, src_ref, *out_refs):
    count, terms = out_refs[0].shape[:2]
    for slot, out_ref in enumerate(out_refs):
        def pick(dest, unused, slot=slot, out_ref=out_ref):
            for term in range(terms):
                out_ref[dest, term] = src_ref[ids_ref[(slot * count + dest) * terms + term]]
            return unused

        lax.fori_loop(0, count, pick, 0)


def gather_pieces(ids, pieces, slots, count):
    norb, rows, lanes = pieces.shape
    block = max(8, rows // 4)
    return pl.pallas_call(
        gather_kernel,
        grid_spec=pltpu.PrefetchScalarGridSpec(
            num_scalar_prefetch=1,
            grid=(rows // block,),
            in_specs=[pl.BlockSpec((norb, block, lanes), lambda i, ids: (0, i, 0))],
            out_specs=[pl.BlockSpec((count, 2, block, lanes), lambda i, ids: (0, 0, i, 0))] * slots,
        ),
        out_shape=[jax.ShapeDtypeStruct((count, 2, rows, lanes), jnp.float32)] * slots,
        cost_estimate=pl.CostEstimate(flops=0, bytes_accessed=8 * norb * rows * lanes, transcendentals=0),
        name="pick_pieces",
    )(ids, pieces)


def scatter_kernel(ids_ref, *refs):
    out_ref = refs[-1]
    out_ref[...] = jnp.zeros_like(out_ref)
    count, terms = refs[0].shape[:2]
    for slot, in_ref in enumerate(refs[:-1]):
        def add(dest, unused, slot=slot, in_ref=in_ref):
            for term in range(terms):
                orbit = ids_ref[(slot * count + dest) * terms + term]
                out_ref[orbit] = out_ref[orbit] + in_ref[dest, term]
            return unused

        lax.fori_loop(0, count, add, 0)


def scatter_pieces(ids, parts, norb):
    count, terms, rows, lanes = parts[0].shape
    block = max(8, rows // 4)
    return pl.pallas_call(
        scatter_kernel,
        grid_spec=pltpu.PrefetchScalarGridSpec(
            num_scalar_prefetch=1,
            grid=(rows // block,),
            in_specs=[pl.BlockSpec((count, terms, block, lanes), lambda i, ids: (0, 0, i, 0))] * len(parts),
            out_specs=pl.BlockSpec((norb, block, lanes), lambda i, ids: (0, i, 0)),
        ),
        out_shape=jax.ShapeDtypeStruct((norb, rows, lanes), jnp.float32),
        cost_estimate=pl.CostEstimate(flops=0, bytes_accessed=8 * norb * rows * lanes, transcendentals=0),
        name="add_pieces",
    )(ids, *parts)


def lane_ids(shape):
    return lax.broadcasted_iota(jnp.int32, shape, len(shape) - 1)


def shift_plane(plane, off_y, off_z):
    shape = plane.shape
    lane = lane_ids(shape)
    row = lax.broadcasted_iota(jnp.int32, shape, 0)
    linear = off_y * B + off_z
    across = jnp.bitwise_and(linear, LANES - 1)
    down = jnp.right_shift(linear, 7)
    turned = pltpu.roll(plane, across, 1)
    near = pltpu.roll(turned, jnp.bitwise_and(down, ROWS - 1), 0)
    far = pltpu.roll(turned, jnp.bitwise_and(down + 1, ROWS - 1), 0)
    moved = jnp.where(lane >= across, near, far)
    from_y = row * 2 + jnp.right_shift(lane, 6) - off_y
    from_z = jnp.bitwise_and(lane, B - 1) - off_z
    inside = (from_y >= 0) & (from_y < B) & (from_z >= 0) & (from_z < B)
    return jnp.where(inside, moved, 0.0)


def operate_plane(before, plane, after):
    shape = plane.shape
    lane = lane_ids(shape)
    row = lax.broadcasted_iota(jnp.int32, shape, 0)
    z = jnp.bitwise_and(lane, B - 1)
    upper_z = jnp.where(z < B - 1, pltpu.roll(plane, LANES - 1, 1), 0.0)
    lower_z = jnp.where(z > 0, pltpu.roll(plane, 1, 1), 0.0)
    half = pltpu.roll(plane, B, 1)
    down = jnp.where(row > 0, pltpu.roll(half, 1, 0), 0.0)
    up = jnp.where(row < ROWS - 1, pltpu.roll(half, ROWS - 1, 0), 0.0)
    beside = (before + after) + (half + jnp.where(lane < B, down, up))
    return 6.0 * plane - beside - upper_z - lower_z


def fold(values):
    return jnp.sum(values.reshape(ROWS // 8, 8, LANES), axis=0)


def total(acc):
    return jnp.sum(acc, axis=(0, 1), keepdims=True)


def solve_kernel(info_ref, *refs):
    chunks = (len(refs) - 6) // 2
    in_refs, out_refs = refs[:chunks], refs[chunks : 2 * chunks]
    wide, partner, direction, resid, image, potential = refs[2 * chunks :]
    count, terms, rows, lanes = in_refs[0].shape
    each = rows // ROWS
    dx, dy, dz = info_ref[0], info_ref[1], info_ref[2]
    keep = jnp.where(info_ref[3] > 0, 1.0, 0.0).astype(jnp.float32)
    edge = jnp.zeros((PAD, ROWS, LANES), jnp.float32)
    wide[pl.ds(0, PAD)] = edge
    wide[pl.ds(PAD + B, PAD)] = edge
    direction[0] = edge[0]
    direction[B + 1] = edge[0]
    none = jnp.zeros((8, LANES), jnp.float32)

    def place(owner, chunk, i):
        return (owner * chunks + chunk) * each + i

    def load(owner, unused):
        for chunk in range(chunks):
            for i in range(each):
                wide[PAD + place(owner, chunk, i)] = in_refs[chunk][owner, 1, pl.ds(i * ROWS, ROWS)]
        return unused

    lax.fori_loop(0, count, load, 0)

    def start(owner, acc):
        for chunk in range(chunks):
            for i in range(each):
                x = place(owner, chunk, i)
                other = shift_plane(wide[PAD + x - dx], dy, dz)
                partner[x] = other
                density = in_refs[chunk][owner, 0, pl.ds(i * ROWS, ROWS)] * other
                direction[x + 1] = density
                resid[x] = density
                acc = acc + fold(density * density)
        return acc

    norm_now = total(lax.fori_loop(0, count, start, none))

    for turn in range(ITERS):
        def apply(block, acc):
            for i in range(STEP):
                x = block * STEP + i
                plane = direction[x + 1]
                result = operate_plane(direction[x], plane, direction[x + 2])
                image[x] = result
                acc = acc + fold(plane * result)
            return acc

        step_len = norm_now / total(lax.fori_loop(0, B // STEP, apply, none))

        if turn == ITERS - 1:
            break

        def advance(block, acc):
            for i in range(STEP):
                x = block * STEP + i
                moved = step_len * direction[x + 1]
                potential[x] = moved if turn == 0 else potential[x] + moved
                left = resid[x] - step_len * image[x]
                resid[x] = left
                acc = acc + fold(left * left)
            return acc

        norm_next = total(lax.fori_loop(0, B // STEP, advance, none))
        ratio = norm_next / norm_now

        def renew(block, unused):
            for i in range(STEP):
                x = block * STEP + i
                direction[x + 1] = resid[x] + ratio * direction[x + 1]
            return unused

        lax.fori_loop(0, B // STEP, renew, 0)
        norm_now = norm_next

    def finish(owner, unused):
        for chunk in range(chunks):
            for i in range(each):
                x = place(owner, chunk, i)
                found = (potential[x] + step_len * direction[x + 1]) * keep
                out_refs[chunk][owner, 0, pl.ds(i * ROWS, ROWS)] = found * partner[x]
                wide[PAD + x] = found * in_refs[chunk][owner, 0, pl.ds(i * ROWS, ROWS)]
        return unused

    lax.fori_loop(0, count, finish, 0)

    def give_back(owner, unused):
        for chunk in range(chunks):
            for i in range(each):
                x = place(owner, chunk, i)
                out_refs[chunk][owner, 1, pl.ds(i * ROWS, ROWS)] = shift_plane(wide[PAD + x + dx], -dy, -dz)
        return unused

    lax.fori_loop(0, count, give_back, 0)


def solve_pair(info, parts):
    box = (B, ROWS, LANES)
    vmem = pl.BlockSpec(memory_space=pltpu.VMEM)
    return pl.pallas_call(
        solve_kernel,
        in_specs=[pl.BlockSpec(memory_space=pltpu.SMEM)] + [vmem] * len(parts),
        out_specs=[vmem] * len(parts),
        out_shape=[jax.ShapeDtypeStruct(p.shape, jnp.float32) for p in parts],
        scratch_shapes=[
            pltpu.VMEM((B + 2 * PAD, ROWS, LANES), jnp.float32),
            pltpu.VMEM(box, jnp.float32),
            pltpu.VMEM((B + 2, ROWS, LANES), jnp.float32),
            pltpu.VMEM(box, jnp.float32),
            pltpu.VMEM(box, jnp.float32),
            pltpu.VMEM(box, jnp.float32),
        ],
        compiler_params=pltpu.CompilerParams(vmem_limit_bytes=32 * 1024 * 1024),
        cost_estimate=pl.CostEstimate(flops=0, bytes_accessed=40 * 1024 * 1024, transcendentals=0),
        name="solve_pair",
    )(info, *parts)


def body(orbitals, anchors, pair_slots):
    grid_count = lax.axis_size("grid")
    owner_count = lax.axis_size("grp") * grid_count
    group_idx = lax.axis_index("grp")
    place_idx = lax.axis_index("grid")
    assignment = deal_evenly(pair_slots, owner_count, PAIR_DEV)
    slots = assignment.shape[1]
    filled = assignment[..., 0] >= 0
    safe_ids = jnp.maximum(assignment, 0)
    group_table = lax.dynamic_slice_in_dim(safe_ids, group_idx * grid_count, grid_count, 0)
    ids = jnp.transpose(group_table, (1, 0, 2)).reshape(-1)
    owner_idx = group_idx * grid_count + place_idx
    own_pairs = safe_ids[owner_idx]
    offsets = anchors[own_pairs[:, 1]] - anchors[own_pairs[:, 0]]
    info = jnp.concatenate([offsets, filled[owner_idx].astype(jnp.int32)[:, None]], axis=1)

    norb_local, cells = orbitals.shape
    stacked = orbitals.reshape(norb_local, cells // LANES, LANES)
    chunks = math.gcd(MOST_CHUNKS, cells // (B * B))
    rows = stacked.shape[1] // chunks
    arrived = [[None] * chunks for _ in range(slots)]
    for chunk in range(chunks):
        pieces = lax.all_gather(stacked[:, chunk * rows : (chunk + 1) * rows], "grp", axis=0, tiled=True)
        outgoing = gather_pieces(ids, pieces, slots, grid_count)
        for slot in range(slots):
            arrived[slot][chunk] = lax.all_to_all(outgoing[slot], "grid", split_axis=0, concat_axis=0, tiled=True)
    returned = []
    for slot in range(slots):
        terms = solve_pair(info[slot], arrived[slot])
        returned.append(
            [lax.all_to_all(t, "grid", split_axis=0, concat_axis=0, tiled=True) for t in terms]
        )
    results = []
    for chunk in range(chunks):
        summed = scatter_pieces(ids, [r[chunk] for r in returned], anchors.shape[0])
        results.append(lax.psum_scatter(summed, "grp", scatter_dimension=0, tiled=True))
    return jnp.concatenate(results, axis=1).reshape(norb_local, cells)


def solution(mesh):
    return jax.shard_map(
        body,
        mesh=mesh,
        in_specs=(P("grp", "grid"), P(), P()),
        out_specs=P("grp", "grid"),
        check_vma=False,
    )
```

profile of v0, /device:TPU:0, one launch (start us, length us, event | category | flops | bytes accessed | tf_op | source)
XLA Modules:
  0.0 387.2 jit_solution(6808570760561516433)
XLA Ops:
  6.5 2.0 copy.29
  8.5 1.6 fusion.4
  10.2 0.7 all-gather.5.cloned.1.call-update
  12.1 0.7 reshape.128.ids_ref
  12.8 52.8 %all-gather.3.cloned.1.call-done.src_ref = f32[64,128,128]{2,1,0:T(8,128)} async-done(((f32[16,128,128]{2,1,0:T(8,128)}), f32[64,128,128]{2,1,0:T(8,128)}) %all-gather.3.cloned.1.call-update) | async-done | bytes 4194320 | tf_op jit(solution)/shard_map/all_gather | solution.py:275
  65.6 5.1 %pick_pieces.2 = (f32[8,2,128,128]{3,2,1,0:T(8,128)}, f32[8,2,128,128]{3,2,1,0:T(8,128)}) custom-call(s32[32]{0:T(128)} %reshape.128.ids_ref, f32[64,128,128]{2,1,0:T(8,128)} %all-gather.3.cloned.1.call-done.src_ref), custom_call_target="tpu_custom_call" | custom-call | bytes 8388608 | tf_op jit(solution)/shard_map/pick_pieces/pallas_call | solution.py:45
  70.7 31.2 %all_to_all.40.refs_0_ = f32[8,2,128,128]{3,2,1,0:T(8,128)S(1)} all-to-all(f32[8,2,128,128]{3,2,1,0:T(8,128)} %get-tuple-element.13), channel_id=1, replica_groups=mesh['grp'=4,'grid'=8] {'grid'}, dimensions={0} | all-to-all | bytes 2097152 | tf_op jit(solution)/shard_map/all_to_all | solution.py:278
  101.8 3.6 all-to-all-start.3
  105.4 14.6 %all-gather.5.cloned.1.call-done.src_ref = f32[64,128,128]{2,1,0:T(8,128)} async-done(((f32[16,128,128]{2,1,0:T(8,128)}), f32[64,128,128]{2,1,0:T(8,128)}) %all-gather.5.cloned.1.call-update) | async-done | bytes 4194320 | tf_op jit(solution)/shard_map/all_gather | solution.py:275
  120.0 5.0 %pick_pieces.3 = (f32[8,2,128,128]{3,2,1,0:T(8,128)}, f32[8,2,128,128]{3,2,1,0:T(8,128)}) custom-call(s32[32]{0:T(128)} %reshape.128.ids_ref, f32[64,128,128]{2,1,0:T(8,128)} %all-gather.5.cloned.1.call-done.src_ref), custom_call_target="tpu_custom_call" | custom-call | bytes 8388608 | tf_op jit(solution)/shard_map/pick_pieces/pallas_call | solution.py:45
  125.1 6.8 %all-to-all-done.3.refs_0_ = f32[8,2,128,128]{3,2,1,0:T(8,128)S(1)} async-done(((f32[8,2,128,128]{3,2,1,0:T(8,128)}), f32[8,2,128,128]{3,2,1,0:T(8,128)S(1)}, u32[]{:S(2)}, u32[]{:S(2)}) %all-to-all-start.3) | async-done | bytes 1048608 | tf_op jit(solution)/shard_map/all_to_all | solution.py:278
  131.9 30.9 %all_to_all.41.refs_1_ = f32[8,2,128,128]{3,2,1,0:T(8,128)} all-to-all(f32[8,2,128,128]{3,2,1,0:T(8,128)} %get-tuple-element.14), channel_id=1, replica_groups=mesh['grp'=4,'grid'=8] {'grid'}, dimensions={0} | all-to-all | bytes 2097152 | tf_op jit(solution)/shard_map/all_to_all | solution.py:278
  162.8 3.6 all-to-all-start.4
  166.9 0.6 gather_fusion.1
  168.1 1.2 copy-done
  169.3 10.6 %solve_pair.2 = (f32[8,2,128,128]{3,2,1,0:T(8,128)S(1)}, f32[8,2,128,128]{3,2,1,0:T(8,128)S(1)}) custom-call(s32[4]{0:T(128)S(1)} %get-tuple-element.28.info_ref, f32[8,2,128,128]{3,2,1,0:T(8,128)S(1)} %all_to_all.40.refs_0_, f32[8,2,128,128]{3,2,1,0:T(8,128)S(1)} %copy-done), custom_call_target="tpu_custom_call" | custom-call | bytes 41943040 | tf_op jit(solution)/shard_map/solve_pair/pallas_call | solution.py:234
  180.0 0.9 copy-done.1
  180.9 1.0 copy-done.3
  181.9 11.0 %all-to-all-done.4.refs_1_ = f32[8,2,128,128]{3,2,1,0:T(8,128)S(1)} async-done(((f32[8,2,128,128]{3,2,1,0:T(8,128)}), f32[8,2,128,128]{3,2,1,0:T(8,128)S(1)}, u32[]{:S(2)}, u32[]{:S(2)}) %all-to-all-start.4) | async-done | bytes 1048608 | tf_op jit(solution)/shard_map/all_to_all | solution.py:278
  192.8 4.2 %all-to-all-start.6 = ((f32[8,2,128,128]{3,2,1,0:T(8,128)}), f32[8,2,128,128]{3,2,1,0:T(8,128)}, u32[]{:S(2)}, u32[]{:S(2)}) async-start(f32[8,2,128,128]{3,2,1,0:T(8,128)} %copy-done.3), calls=%async_computation.7 | async-start | bytes 2097152 | tf_op jit(solution)/shard_map/all_to_all | solution.py:283
  197.1 10.6 %solve_pair.3 = (f32[8,2,128,128]{3,2,1,0:T(8,128)S(1)}, f32[8,2,128,128]{3,2,1,0:T(8,128)S(1)}) custom-call(s32[4]{0:T(128)S(1)} %get-tuple-element.27.info_ref, f32[8,2,128,128]{3,2,1,0:T(8,128)S(1)} %all-to-all-done.3.refs_0_, f32[8,2,128,128]{3,2,1,0:T(8,128)S(1)} %all-to-all-done.4.refs_1_), custom_call_target="tpu_custom_call" | custom-call | bytes 41943040 | tf_op jit(solution)/shard_map/solve_pair/pallas_call | solution.py:234
  207.8 1.0 copy-done.4
  208.7 14.9 %all-to-all-done.6.refs_0_ = f32[8,2,128,128]{3,2,1,0:T(8,128)} async-done(((f32[8,2,128,128]{3,2,1,0:T(8,128)}), f32[8,2,128,128]{3,2,1,0:T(8,128)}, u32[]{:S(2)}, u32[]{:S(2)}) %all-to-all-start.6) | async-done | bytes 1048608 | tf_op jit(solution)/shard_map/all_to_all | solution.py:283
  223.7 30.8 %all_to_all.42.refs_1_ = f32[8,2,128,128]{3,2,1,0:T(8,128)} all-to-all(f32[8,2,128,128]{3,2,1,0:T(8,128)} %copy-done.4), channel_id=1, replica_groups=mesh['grp'=4,'grid'=8] {'grid'}, dimensions={0} | all-to-all | bytes 2097152 | tf_op jit(solution)/shard_map/all_to_all | solution.py:283
  254.4 5.3 %add_pieces.3 = f32[64,128,128]{2,1,0:T(8,128)} custom-call(s32[32]{0:T(128)} %reshape.128.ids_ref, f32[8,2,128,128]{3,2,1,0:T(8,128)} %all-to-all-done.6.refs_0_, f32[8,2,128,128]{3,2,1,0:T(8,128)} %all_to_all.42.refs_1_), custom_call_target="tpu_custom_call" | custom-call | bytes 8388608 | tf_op jit(solution)/shard_map/add_pieces/pallas_call | solution.py:76
  259.8 1.1 copy-done.2
  261.0 29.7 %all_to_all.43.refs_0_ = f32[8,2,128,128]{3,2,1,0:T(8,128)} all-to-all(f32[8,2,128,128]{3,2,1,0:T(8,128)S(1)} %copy-done.2), channel_id=1, replica_groups=mesh['grp'=4,'grid'=8] {'grid'}, dimensions={0} | all-to-all | bytes 2097152 | tf_op jit(solution)/shard_map/all_to_all | solution.py:283
  290.6 29.7 %all_to_all.44.refs_1_ = f32[8,2,128,128]{3,2,1,0:T(8,128)} all-to-all(f32[8,2,128,128]{3,2,1,0:T(8,128)S(1)} %get-tuple-element.18), channel_id=1, replica_groups=mesh['grp'=4,'grid'=8] {'grid'}, dimensions={0} | all-to-all | bytes 2097152 | tf_op jit(solution)/shard_map/all_to_all | solution.py:283
  320.3 5.4 %add_pieces.2 = f32[64,128,128]{2,1,0:T(8,128)} custom-call(s32[32]{0:T(128)} %reshape.128.ids_ref, f32[8,2,128,128]{3,2,1,0:T(8,128)} %all_to_all.43.refs_0_, f32[8,2,128,128]{3,2,1,0:T(8,128)} %all_to_all.44.refs_1_), custom_call_target="tpu_custom_call" | custom-call | bytes 8388608 | tf_op jit(solution)/shard_map/add_pieces/pallas_call | solution.py:76
  325.8 50.7 %reduce-scatter.3.cloned.1.call-done = f32[16,128,128]{2,1,0:T(8,128)} async-done(((f32[64,128,128]{2,1,0:T(8,128)}), f32[16,128,128]{2,1,0:T(8,128)}) %reduce-scatter.3.cloned.1.call-update) | async-done | bytes 1048592 | tf_op jit(solution)/shard_map/reduce_scatter | solution.py:288
  376.4 1.7 pad_maximum_fusion
  378.1 2.5 copy.32
  (43 shorter events, 2.5 us)
Async XLA Ops:
  6.5 59.1 %all-gather.3.cloned.1.call-start = ((), (), s32[]{:S(2)}) async-start(), calls=%async_computation.10 | async-start | bytes 5242880 | tf_op jit(solution)/shard_map/all_gather | solution.py:275
  10.1 0.9 copy-start.5
  10.1 109.9 %all-gather.5.cloned.1.call-start = ((), (), s32[]{:S(2)}) async-start(), calls=%async_computation.11 | async-start | bytes 5242880 | tf_op jit(solution)/shard_map/all_gather | solution.py:275
  101.8 30.1 %all-to-all-start.3 = ((f32[8,2,128,128]{3,2,1,0:T(8,128)}), f32[8,2,128,128]{3,2,1,0:T(8,128)S(1)}, u32[]{:S(2)}, u32[]{:S(2)}) async-start(f32[8,2,128,128]{3,2,1,0:T(8,128)} %get-tuple-element.16), calls=%async_computation.3 | async-start | bytes 2097152 | tf_op jit(solution)/shard_map/all_to_all | solution.py:278
  131.9 34.5 %copy-start.6 = (s32[64,3]{0,1:T(4,128)S(1)}, s32[64,3]{0,1:T(4,128)}, u32[]{:S(2)}) copy-start(s32[64,3]{0,1:T(4,128)} %param.4) | copy-start | bytes 2308
  162.8 30.1 %all-to-all-start.4 = ((f32[8,2,128,128]{3,2,1,0:T(8,128)}), f32[8,2,128,128]{3,2,1,0:T(8,128)S(1)}, u32[]{:S(2)}, u32[]{:S(2)}) async-start(f32[8,2,128,128]{3,2,1,0:T(8,128)} %get-tuple-element.17), calls=%async_computation.4 | async-start | bytes 2097152 | tf_op jit(solution)/shard_map/all_to_all | solution.py:278
  168.1 1.2 copy-start
  180.0 1.0 copy-start.1
  180.9 1.0 copy-start.3
  192.8 30.8 %all-to-all-start.6 = ((f32[8,2,128,128]{3,2,1,0:T(8,128)}), f32[8,2,128,128]{3,2,1,0:T(8,128)}, u32[]{:S(2)}, u32[]{:S(2)}) async-start(f32[8,2,128,128]{3,2,1,0:T(8,128)} %copy-done.3), calls=%async_computation.7 | async-start | bytes 2097152 | tf_op jit(solution)/shard_map/all_to_all | solution.py:283
  197.1 128.7 %reduce-scatter.5.cloned.1.call-start = ((), (), s32[]{:S(2)}) async-start(), calls=%async_computation.13 | async-start | bytes 5242880 | tf_op jit(solution)/shard_map/reduce_scatter | solution.py:288
  207.8 1.0 copy-start.4
  259.7 1.2 copy-start.2
  259.8 116.7 %reduce-scatter.3.cloned.1.call-start = ((), (), s32[]{:S(2)}) async-start(), calls=%async_computation.12 | async-start | bytes 5242880 | tf_op jit(solution)/shard_map/reduce_scatter | solution.py:288
Sparse Core Ops, SparseCore 0:
  10.2 55.3 all-gather.2
  67.4 52.5 all-gather.4
  259.9 50.5 reduce-scatter.4
  325.9 50.5 reduce-scatter.2
where the time goes:
time: 388 us; the launch traced here: 387 us
  waiting for transfers between devices  152 us (39%)
  blocking collectives  152 us (39%)
  Pallas kernels  42 us (11%)
  local copies, waits for them, and re-layouts  14 us (4%)
  between operations  13.3 us (3%)
  starting transfers between devices  11.5 us (3%)
    all_to_all x3, blocking collectives, body(): lax.all_to_all(t, 'grid', split_axis=0, concat_axis=0, tiled=True)  90.1 us
    all_gather x2, waiting for transfers between devices, body(): lax.all_gather(stacked[:, chunk * rows:(chunk + 1) * rows], 'grp', axis=0...  67.5 us
    all_to_all x2, blocking collectives, body(): lax.all_to_all(outgoing[slot], 'grid', split_axis=0, concat_axis=0, tiled...  62.1 us
    reduce_scatter x2, waiting for transfers between devices, body(): lax.psum_scatter(summed, 'grp', scatter_dimension=0, tiled=True)  50.7 us
    pallas_call x2, Pallas kernels, solve_pair(): pl.pallas_call(solve_kernel, in_specs=[pl.BlockSpec(memory_space=pltpu.SM...  21.2 us
    all_to_all x2, waiting for transfers between devices, body(): lax.all_to_all(outgoing[slot], 'grid', split_axis=0, concat_axis=0, tiled...  17.8 us
    all_to_all x1, waiting for transfers between devices, body(): lax.all_to_all(t, 'grid', split_axis=0, concat_axis=0, tiled=True)  14.9 us
    pallas_call x2, Pallas kernels, scatter_pieces(): pl.pallas_call(scatter_kernel, grid_spec=pltpu.PrefetchScalarGridSpec(num...  10.7 us
  transfers between devices with their start and end apart: 7, of which 6 were waited for; matrix products, arithmetic and copies ran while one was open for 1% of the time, Pallas kernels for 9%

commit v1 on v0

--- a/solution.py
+++ b/solution.py
@@ -1,3 +1,4 @@
+import functools
 import math
 
 import jax
@@ -250,7 +251,7 @@
     )(info, *parts)
 
 
-def body(orbitals, anchors, pair_slots):
+def owner_body(orbitals, anchors, pair_slots):
     grid_count = lax.axis_size("grid")
     owner_count = lax.axis_size("grp") * grid_count
     group_idx = lax.axis_index("grp")
@@ -289,9 +290,748 @@
     return jnp.concatenate(results, axis=1).reshape(norb_local, cells)
 
 
+MESH = pl.DeviceIdType.MESH
+HALO = 3
+WAVES = 4
+SUB = 8
+
+
+def remote(src, dst, send_sem, recv_sem, device):
+    return pltpu.make_async_remote_copy(
+        src_ref=src, dst_ref=dst, send_sem=send_sem, recv_sem=recv_sem, device_id=device, device_id_type=MESH
+    )
+
+
+def spot():
+    grp = lax.axis_index("grp")
+    place = lax.axis_index("grid")
+    across = grp + 1 - 2 * lax.rem(grp, 2)
+    along = lax.rem(grp + 2, 4)
+    corner = lax.rem(across + 2, 4)
+    return grp, place, across, along, corner
+
+
+def greet(chips):
+    grp, place, across, along, unused = spot()
+    chip = place // 2
+    core = lax.rem(place, 2)
+    barrier = pltpu.get_barrier_semaphore()
+    for device in ((across, place), (along, place), (grp, 2 * chip + 1 - core)):
+        pl.semaphore_signal(barrier, inc=1, device_id=device, device_id_type=MESH)
+
+    @pl.when(chip > 0)
+    def below():
+        pl.semaphore_signal(barrier, inc=1, device_id=(grp, place - 2), device_id_type=MESH)
+
+    @pl.when(chip < chips - 1)
+    def above():
+        pl.semaphore_signal(barrier, inc=1, device_id=(grp, place + 2), device_id_type=MESH)
+
+    ends = jnp.where(chip > 0, 1, 0) + jnp.where(chip < chips - 1, 1, 0)
+    pl.semaphore_wait(barrier, 3 + ends)
+
+
+class Relay:
+    def __init__(self, wins, send_sem, recv_sem, signs, chips):
+        self.wins, self.send_sem, self.recv_sem, self.signs, self.chips = wins, send_sem, recv_sem, signs, chips
+        self.grp, self.place = lax.axis_index("grp"), lax.axis_index("grid")
+        self.chip = self.place // 2
+        self.core = lax.rem(self.place, 2)
+        self.half = wins[0].shape[0] // 2
+        self.planes = wins[0].shape[1] // 6
+
+    def offset(self, sign, hop):
+        return 2 * self.planes * (2 - hop if sign > 0 else hop)
+
+    def region(self, chunk, side, hop, core):
+        start = self.offset(self.signs[side], hop) + self.planes * core
+        return self.wins[chunk].at[pl.ds(side * self.half, self.half), pl.ds(start, self.planes)]
+
+    def comes(self, side, hop):
+        source = self.chip - self.signs[side] * hop
+        return source >= 0 if self.signs[side] > 0 else source < self.chips
+
+    def goes(self, side, hop):
+        source = self.chip + self.signs[side] - self.signs[side] * hop
+        if self.signs[side] > 0:
+            return (self.chip + 1 < self.chips) & (source >= 0)
+        return (self.chip - 1 >= 0) & (source < self.chips)
+
+    def onward(self, chunk, side, hop):
+        here = self.region(chunk, side, hop - 1, self.core)
+        there = self.region(chunk, side, hop, self.core)
+        return remote(
+            here, there, self.send_sem.at[chunk, side, hop - 1], self.recv_sem.at[chunk, side, hop - 1],
+            (self.grp, self.place + 2 * self.signs[side]),
+        )
+
+    def arriving(self, chunk, side, hop):
+        there = self.region(chunk, side, hop, self.core)
+        return remote(
+            there, there, self.send_sem.at[chunk, side, hop - 1], self.recv_sem.at[chunk, side, hop - 1],
+            (self.grp, self.place + 2 * self.signs[side]),
+        )
+
+    def beside(self, chunk, side, hop, core):
+        part = self.region(chunk, side, hop, core)
+        return remote(
+            part, part, self.send_sem.at[chunk, side, 2 + hop], self.recv_sem.at[chunk, side, 2 + hop],
+            (self.grp, 2 * self.chip + 1 - self.core),
+        )
+
+    def clear(self):
+        for side in range(2):
+            for hop in (1, 2):
+                start = self.offset(self.signs[side], hop)
+
+                @pl.when(jnp.logical_not(self.comes(side, hop)))
+                def fill(side=side, start=start):
+                    for win in self.wins:
+                        def zero(slot, unused, win=win):
+                            win[slot, pl.ds(start, 2 * self.planes)] = jnp.zeros(
+                                (2 * self.planes,) + win.shape[2:], jnp.float32
+                            )
+                            return unused
+
+                        lax.fori_loop(side * self.half, (side + 1) * self.half, zero, 0)
+
+    def begin(self, chunk):
+        for side in range(2):
+            self.beside(chunk, side, 0, self.core).start()
+
+            @pl.when(self.goes(side, 1))
+            def go(side=side):
+                self.onward(chunk, side, 1).start()
+
+    def first(self, chunk):
+        for side in range(2):
+            @pl.when(self.comes(side, 1))
+            def got(side=side):
+                self.arriving(chunk, side, 1).wait_recv()
+                self.beside(chunk, side, 1, self.core).start()
+
+            @pl.when(self.goes(side, 2))
+            def go(side=side):
+                self.onward(chunk, side, 2).start()
+
+    def second(self, chunk):
+        for side in range(2):
+            @pl.when(self.comes(side, 2))
+            def got(side=side):
+                self.arriving(chunk, side, 2).wait_recv()
+                self.beside(chunk, side, 2, self.core).start()
+
+    def settle(self, chunk):
+        for side in range(2):
+            self.beside(chunk, side, 0, 1 - self.core).wait_recv()
+            for hop in (1, 2):
+                @pl.when(self.comes(side, hop))
+                def got(side=side, hop=hop):
+                    self.beside(chunk, side, hop, 1 - self.core).wait_recv()
+
+    def drain(self):
+        for chunk in range(len(self.wins)):
+            for side in range(2):
+                self.beside(chunk, side, 0, self.core).wait_send()
+                for hop in (1, 2):
+                    @pl.when(self.comes(side, hop))
+                    def sent(chunk=chunk, side=side, hop=hop):
+                        self.beside(chunk, side, hop, self.core).wait_send()
+
+                    @pl.when(self.goes(side, hop))
+                    def passed(chunk=chunk, side=side, hop=hop):
+                        self.onward(chunk, side, hop).wait_send()
+
+
+def bring_kernel(chips, tbl, orb, moved, fixed, *scratch):
+    count = moved.shape[0]
+    pools, wins = scratch[:count], scratch[count : 2 * count]
+    own_sem, xy_send, xy_recv, z_send, z_recv = scratch[2 * count :]
+    grp, place, across, along, corner = spot()
+    core = lax.rem(place, 2)
+    norb, planes = orb.shape[:2]
+    part = norb // 2
+    slots = moved.shape[1]
+    relay = Relay(wins, z_send, z_recv, (1, -1), chips)
+
+    def block(chunk, owner, start, size):
+        return pools[chunk].at[pl.ds(owner * norb + start, size)]
+
+    def stage(chunk):
+        return pltpu.make_async_copy(
+            orb.at[:, :, pl.ds(chunk * SUB, SUB)], block(chunk, grp, 0, norb), own_sem.at[chunk]
+        )
+
+    def hop(chunk, kind, owner, start, size, target):
+        ref = block(chunk, owner, start, size)
+        return remote(ref, ref, xy_send.at[chunk, kind], xy_recv.at[chunk, kind], (target, place))
+
+    def direct(chunk, owners):
+        return hop(chunk, 0, owners[0], 0, norb, across), hop(chunk, 1, owners[1], 0, norb, along)
+
+    def turned(chunk, owners):
+        return hop(chunk, 2, owners[0], 0, part, along), hop(chunk, 3, owners[1], part, part, across)
+
+    for chunk in range(count):
+        stage(chunk).start()
+    greet(chips)
+    relay.clear()
+
+    def send_own(chunk):
+        stage(chunk).wait()
+        for copy in direct(chunk, (grp, grp)):
+            copy.start()
+
+    send_own(0)
+    send_own(1)
+    for step in range(count + 4):
+        if step < count:
+            for copy in direct(step, (across, along)):
+                copy.wait_recv()
+            for copy in turned(step, (across, along)):
+                copy.start()
+            if step + 2 < count:
+                send_own(step + 2)
+        chunk = step - 1
+        if 0 <= chunk < count:
+            for copy in turned(chunk, (corner, corner)):
+                copy.wait_recv()
+            for side in range(2):
+                start = relay.offset(relay.signs[side], 0) + planes * core
+
+                def pick(slot, unused, start=start, chunk=chunk):
+                    wins[chunk][slot, pl.ds(start, planes)] = pools[chunk][tbl[0, slot]]
+                    fixed[chunk, slot] = pools[chunk][tbl[1, slot]]
+                    return unused
+
+                lax.fori_loop(side * (slots // 2), (side + 1) * (slots // 2), pick, 0)
+            relay.begin(chunk)
+        chunk = step - 2
+        if 0 <= chunk < count:
+            relay.first(chunk)
+        chunk = step - 3
+        if 0 <= chunk < count:
+            relay.second(chunk)
+        chunk = step - 4
+        if 0 <= chunk < count:
+            relay.settle(chunk)
+
+            def choose(slot, unused, chunk=chunk):
+                first = tbl[2, slot] + planes * core
+                for plane in range(planes):
+                    moved[chunk, slot, plane] = wins[chunk][slot, first + plane]
+                return unused
+
+            lax.fori_loop(0, slots, choose, 0)
+    for chunk in range(count):
+        for copy in direct(chunk, (grp, grp)) + turned(chunk, (across, along)):
+            copy.wait_send()
+    relay.drain()
+
+
+def bring(table, stacked, slots, groups, chips):
+    norb, planes, rows, lanes = stacked.shape
+    chunks = rows // SUB
+    vmem = pl.BlockSpec(memory_space=pltpu.VMEM)
+    dma = pltpu.SemaphoreType.DMA
+    shape = jax.ShapeDtypeStruct((chunks, slots, planes, SUB, lanes), jnp.float32)
+    return pl.pallas_call(
+        functools.partial(bring_kernel, chips),
+        in_specs=[pl.BlockSpec(memory_space=pltpu.SMEM), pl.BlockSpec(memory_space=pl.ANY)],
+        out_specs=[vmem, vmem],
+        out_shape=[shape, shape],
+        scratch_shapes=[pltpu.VMEM((groups * norb, planes, SUB, lanes), jnp.float32)] * chunks
+        + [pltpu.VMEM((slots, 6 * planes, SUB, lanes), jnp.float32)] * chunks
+        + [dma((chunks,)), dma((chunks, 4)), dma((chunks, 4)), dma((chunks, 2, 5)), dma((chunks, 2, 5))],
+        compiler_params=pltpu.CompilerParams(
+            collective_id=0, has_side_effects=True, vmem_limit_bytes=48 * 1024 * 1024
+        ),
+        name="bring",
+    )(table, stacked)
+
+
+def pair_kernel(tbl, moved, fixed, dens, partner):
+    slot = pl.program_id(0)
+    second = tbl[3, slot] > 0
+    dy, dz = tbl[4, slot], tbl[5, slot]
+
+    for x in range(moved.shape[2]):
+        left = moved[:, 0, x].reshape(ROWS, LANES)
+        right = fixed[:, 0, x].reshape(ROWS, LANES)
+        other = shift_plane(jnp.where(second, left, right), dy, dz)
+        dens[0, x] = jnp.where(second, right, left) * other
+        partner[0, x] = other
+
+
+def pair_up(table, moved, fixed):
+    chunks, slots, planes, sub, lanes = moved.shape
+    tiled = pl.BlockSpec((chunks, 1, planes, sub, lanes), lambda i, t: (0, i, 0, 0, 0))
+    plain = pl.BlockSpec((1, planes, ROWS, lanes), lambda i, t: (i, 0, 0, 0))
+    shape = jax.ShapeDtypeStruct((slots, planes, ROWS, lanes), jnp.float32)
+    return pl.pallas_call(
+        pair_kernel,
+        grid_spec=pltpu.PrefetchScalarGridSpec(
+            num_scalar_prefetch=1, grid=(slots,), in_specs=[tiled, tiled], out_specs=[plain, plain]
+        ),
+        out_shape=[shape, shape],
+        name="pair_up",
+    )(table, moved, fixed)
+
+
+def inner(plane):
+    shape = plane.shape
+    lane = lane_ids(shape)
+    row = lax.broadcasted_iota(jnp.int32, shape, 0)
+    z = jnp.bitwise_and(lane, B - 1)
+    upper_z = jnp.where(z < B - 1, pltpu.roll(plane, LANES - 1, 1), 0.0)
+    lower_z = jnp.where(z > 0, pltpu.roll(plane, 1, 1), 0.0)
+    half = pltpu.roll(plane, B, 1)
+    down = jnp.where(row > 0, pltpu.roll(half, 1, 0), 0.0)
+    up = jnp.where(row < ROWS - 1, pltpu.roll(half, ROWS - 1, 0), 0.0)
+    return 6.0 * plane - ((half + jnp.where(lane < B, down, up)) + (upper_z + lower_z))
+
+
+def krylov_weights(m):
+    a0 = m[0] / m[1]
+    rr1 = a0 * a0 * m[2] - m[0]
+    p, q = 1.0 + rr1 / m[0], -a0
+    a1 = rr1 / (p * p * m[1] + 2.0 * p * q * m[2] + q * q * m[3])
+    s1, s2 = -a0 - a1 * p, -a1 * q
+    rr2 = (m[0] + s1 * s1 * m[2] + s2 * s2 * m[4]) + 2.0 * (s1 * m[1] + s2 * m[2] + s1 * s2 * m[3])
+    b1 = rr2 / rr1
+    e0, e1, e2 = 1.0 + b1 * p, s1 + b1 * q, s2
+    bend = e0 * e0 * m[1] + e1 * e1 * m[3] + e2 * e2 * m[5]
+    a2 = rr2 / (bend + 2.0 * (e0 * e1 * m[2] + e0 * e2 * m[3] + e1 * e2 * m[4]))
+    return a0 + a1 * p + a2 * e0, a1 * q + a2 * e1, a2 * e2
+
+
+def solve_slabs_kernel(places, tbl, dens, pot, wide, one, two, sums, gathered, weights, h_send, h_recv, s_send, s_recv):
+    grp, place = lax.axis_index("grp"), lax.axis_index("grid")
+    slots, planes = dens.shape[:2]
+    first, last = HALO, HALO + planes - 1
+    each = slots // WAVES
+    barrier = pltpu.get_barrier_semaphore()
+    for step in range(1, places):
+        pl.semaphore_signal(
+            barrier, inc=1, device_id=(grp, lax.rem(place + step, places)), device_id_type=MESH
+        )
+    pl.semaphore_wait(barrier, places - 1)
+
+    def rise(wave):
+        return remote(
+            dens.at[pl.ds(wave * each, each), pl.ds(planes - HALO, HALO)],
+            wide.at[pl.ds(wave * each, each), pl.ds(0, HALO)],
+            h_send.at[wave, 0], h_recv.at[wave, 0], (grp, lax.rem(place + 1, places)),
+        )
+
+    def sink(wave):
+        return remote(
+            dens.at[pl.ds(wave * each, each), pl.ds(0, HALO)],
+            wide.at[pl.ds(wave * each, each), pl.ds(HALO + planes, HALO)],
+            h_send.at[wave, 1], h_recv.at[wave, 1], (grp, lax.rem(place + places - 1, places)),
+        )
+
+    lowest, highest = place == 0, place == places - 1
+    for wave in range(WAVES):
+        @pl.when(jnp.logical_not(highest))
+        def send_up(wave=wave):
+            rise(wave).start()
+
+        @pl.when(jnp.logical_not(lowest))
+        def send_down(wave=wave):
+            sink(wave).start()
+
+    blank = jnp.zeros((HALO, ROWS, LANES), jnp.float32)
+
+    def copy_in(slot, unused):
+        wide[slot, pl.ds(HALO, planes)] = dens[slot]
+        one[slot, 1] = blank[0]
+        one[slot, last + 3] = blank[0]
+        one[slot, 0] = blank[0]
+        return unused
+
+    lax.fori_loop(0, slots, copy_in, 0)
+
+    @pl.when(lowest)
+    def no_below():
+        def fill(slot, unused):
+            wide[slot, pl.ds(0, HALO)] = blank
+            return unused
+
+        lax.fori_loop(0, slots, fill, 0)
+
+    @pl.when(highest)
+    def no_above():
+        def fill(slot, unused):
+            wide[slot, pl.ds(HALO + planes, HALO)] = blank
+            return unused
+
+        lax.fori_loop(0, slots, fill, 0)
+
+    lane = lax.broadcasted_iota(jnp.int32, (1, LANES), 1)
+    none = jnp.zeros((8, LANES), jnp.float32)
+
+    def row_of(parts):
+        row = jnp.zeros((1, LANES), jnp.float32)
+        for at, part in parts:
+            row = row + jnp.where(lane == at, total(part), 0.0)
+        return row
+
+    def work(slot, unused):
+        low, high = tbl[6, slot], tbl[6, slot] + B
+
+        def live(e):
+            x = planes * place + e - HALO
+            return jnp.where((x >= low) & (x < high), 1.0, 0.0).astype(jnp.float32)
+
+        m0, m1, m2, m3, m4, m5 = none, none, none, none, none, none
+        for e in range(first - 1, last + 3):
+            value = live(e) * (inner(wide[slot, e]) - (wide[slot, e - 1] + wide[slot, e + 1]))
+            one[slot, e] = value
+            if first <= e <= last:
+                source = wide[slot, e]
+                m0 = m0 + fold(source * source)
+                m1 = m1 + fold(source * value)
+                m2 = m2 + fold(value * value)
+        bent = None
+        for e in range(first, last + 2):
+            value = live(e) * (inner(one[slot, e]) - (one[slot, e - 1] + one[slot, e + 1]))
+            two[slot, e] = value
+            if e > first:
+                m5 = m5 - 2.0 * fold(value * two[slot, e - 1])
+            if e <= last:
+                m3 = m3 + fold(one[slot, e] * value)
+                m4 = m4 + fold(value * value)
+                m5 = m5 + fold(value * inner(value))
+        sums[pl.ds(slot, 1)] = row_of(enumerate((m0, m1, m2, m3, m4, m5)))
+        return unused
+
+    def rim(slot, spots, pairs):
+        low, high = tbl[6, slot], tbl[6, slot] + B
+        m2, m3, m4, m5 = none, none, none, none
+        for e, fresh in spots:
+            if fresh:
+                x = planes * place + e - HALO
+                alive = jnp.where((x >= low) & (x < high), 1.0, 0.0).astype(jnp.float32)
+                two[slot, e] = alive * (inner(one[slot, e]) - (one[slot, e - 1] + one[slot, e + 1]))
+        for e, fresh in spots:
+            value, before = two[slot, e], one[slot, e]
+            m2 = m2 + fold(before * before)
+            m3 = m3 + fold(before * value)
+            m4 = m4 + fold(value * value)
+            m5 = m5 + fold(value * inner(value))
+        for e in pairs:
+            m5 = m5 - 2.0 * fold(two[slot, e] * two[slot, e + 1])
+        sums[pl.ds(slot, 1)] = sums[pl.ds(slot, 1)] + row_of(((2, m2), (3, m3), (4, m4), (5, m5)))
+
+    for wave in range(WAVES):
+        @pl.when(jnp.logical_not(lowest))
+        def got_below(wave=wave):
+            rise(wave).wait_recv()
+
+        @pl.when(jnp.logical_not(highest))
+        def got_above(wave=wave):
+            sink(wave).wait_recv()
+
+        lax.fori_loop(wave * each, (wave + 1) * each, work, 0)
+
+    @pl.when(lowest)
+    def rim_below():
+        def go(slot, unused):
+            rim(slot, ((first - 2, True), (first - 1, True)), (first - 2, first - 1))
+            return unused
+
+        lax.fori_loop(0, slots, go, 0)
+
+    @pl.when(highest)
+    def rim_above():
+        def go(slot, unused):
+            rim(slot, ((last + 1, False), (last + 2, True)), (last + 1,))
+            return unused
+
+        lax.fori_loop(0, slots, go, 0)
+
+    def tell(step):
+        return remote(
+            sums, gathered.at[place], s_send.at[step - 1], s_recv.at[step - 1],
+            (grp, lax.rem(place + step, places)),
+        )
+
+    def hear(step):
+        source = lax.rem(place + places - step, places)
+        return remote(
+            sums, gathered.at[source], s_send.at[step - 1], s_recv.at[step - 1],
+            (grp, lax.rem(place + step, places)),
+        )
+
+    for step in range(1, places):
+        tell(step).start()
+    gathered[place] = sums[...]
+    for step in range(1, places):
+        hear(step).wait_recv()
+    whole = gathered[0]
+    for at in range(1, places):
+        whole = whole + gathered[at]
+    lanes = lax.broadcasted_iota(jnp.int32, whole.shape, 1)
+    moments = [jnp.sum(jnp.where(lanes == at, whole, 0.0), axis=1, keepdims=True) for at in range(6)]
+    for at, weight in enumerate(krylov_weights(moments)):
+        weights[at] = jnp.broadcast_to(weight, whole.shape)
+
+    def finish(slot, unused):
+        w0, w1, w2 = [weights[at, pl.ds(slot, 1)] for at in range(3)]
+        for x in range(planes):
+            e = x + HALO
+            pot[slot, x] = w0 * wide[slot, e] + w1 * one[slot, e] + w2 * two[slot, e]
+        return unused
+
+    lax.fori_loop(0, slots, finish, 0)
+    for wave in range(WAVES):
+        @pl.when(jnp.logical_not(highest))
+        def sent_up(wave=wave):
+            rise(wave).wait_send()
+
+        @pl.when(jnp.logical_not(lowest))
+        def sent_down(wave=wave):
+            sink(wave).wait_send()
+
+    for step in range(1, places):
+        tell(step).wait_send()
+
+
+def solve_slabs(table, dens, places):
+    slots, planes, rows, lanes = dens.shape
+    vmem = pl.BlockSpec(memory_space=pltpu.VMEM)
+    dma = pltpu.SemaphoreType.DMA
+    tall = pltpu.VMEM((slots, planes + 2 * HALO, rows, lanes), jnp.float32)
+    return pl.pallas_call(
+        functools.partial(solve_slabs_kernel, places),
+        in_specs=[pl.BlockSpec(memory_space=pltpu.SMEM), vmem],
+        out_specs=vmem,
+        out_shape=jax.ShapeDtypeStruct(dens.shape, jnp.float32),
+        scratch_shapes=[
+            tall, tall, tall,
+            pltpu.VMEM((slots, lanes), jnp.float32),
+            pltpu.VMEM((places, slots, lanes), jnp.float32),
+            pltpu.VMEM((3, slots, lanes), jnp.float32),
+            dma((WAVES, 2)), dma((WAVES, 2)), dma((places - 1,)), dma((places - 1,)),
+        ],
+        compiler_params=pltpu.CompilerParams(
+            collective_id=1, has_side_effects=True, vmem_limit_bytes=40 * 1024 * 1024
+        ),
+        name="solve_slabs",
+    )(table, dens)
+
+
+def term_kernel(tbl, pot, partner, moved, fixed, going, staying):
+    slot = pl.program_id(0)
+    second = tbl[3, slot] > 0
+    dy, dz = tbl[4, slot], tbl[5, slot]
+    chunks = going.shape[0]
+    for x in range(pot.shape[1]):
+        found = pot[0, x]
+        left = moved[:, 0, x].reshape(ROWS, LANES)
+        right = fixed[:, 0, x].reshape(ROWS, LANES)
+        term_a = found * partner[0, x]
+        term_b = shift_plane(found * jnp.where(second, right, left), -dy, -dz)
+        going[:, 0, x] = jnp.where(second, term_b, term_a).reshape(chunks, SUB, LANES)
+        staying[:, 0, x] = jnp.where(second, term_a, term_b).reshape(chunks, SUB, LANES)
+
+
+def make_terms(table, pot, partner, moved, fixed):
+    chunks, slots, planes, sub, lanes = moved.shape
+    tiled = pl.BlockSpec((chunks, 1, planes, sub, lanes), lambda i, t: (0, i, 0, 0, 0))
+    plain = pl.BlockSpec((1, planes, ROWS, lanes), lambda i, t: (i, 0, 0, 0))
+    shape = jax.ShapeDtypeStruct(moved.shape, jnp.float32)
+    return pl.pallas_call(
+        term_kernel,
+        grid_spec=pltpu.PrefetchScalarGridSpec(
+            num_scalar_prefetch=1, grid=(slots,), in_specs=[plain, plain, tiled, tiled], out_specs=[tiled, tiled]
+        ),
+        out_shape=[shape, shape],
+        name="make_terms",
+    )(table, pot, partner, moved, fixed)
+
+
+def hand_back_kernel(chips, tbl, last, going, staying, out, *scratch):
+    count, slots = going.shape[:2]
+    wins, chains, outs1, outs2, ins1, ins2 = [scratch[i * count : (i + 1) * count] for i in range(6)]
+    xy_send, xy_recv, z_send, z_recv = scratch[6 * count :]
+    grp, place, across, along, corner = spot()
+    core = lax.rem(place, 2)
+    norb, planes = out.shape[:2]
+    part = norb // 2
+    relay = Relay(wins, z_send, z_recv, (-1, 1), chips)
+    greet(chips)
+    relay.clear()
+
+    def start(chunk):
+        for side in range(2):
+            at = relay.offset(relay.signs[side], 0) + planes * core
+
+            def place_in(slot, unused, at=at):
+                wins[chunk][slot, pl.ds(at, planes)] = going[chunk, slot]
+                return unused
+
+            lax.fori_loop(side * (slots // 2), (side + 1) * (slots // 2), place_in, 0)
+        relay.begin(chunk)
+
+    def swap(chunk, kind):
+        src = (outs1 if kind < 2 else outs2)[chunk].at[kind % 2]
+        dst = (ins1 if kind < 2 else ins2)[chunk].at[kind % 2]
+        target = (across, along, along, across)[kind]
+        return remote(src, dst, xy_send.at[chunk, kind], xy_recv.at[chunk, kind], (target, place))
+
+    start(0)
+    start(1)
+    for step in range(count + 4):
+        if step < count:
+            relay.first(step)
+            if step + 2 < count:
+                start(step + 2)
+        chunk = step - 1
+        if 0 <= chunk < count:
+            relay.second(chunk)
+        chunk = step - 2
+        if 0 <= chunk < count:
+            relay.settle(chunk)
+            chain = chains[chunk]
+            chain[2 * slots] = jnp.zeros(chain.shape[1:], jnp.float32)
+
+            def link_fixed(slot, unused, chain=chain, chunk=chunk):
+                chain[slot] = staying[chunk, slot] + chain[tbl[8, slot]]
+                return unused
+
+            def link_moved(slot, unused, chain=chain, chunk=chunk):
+                first = tbl[7, slot] + planes * core
+                for plane in range(planes):
+                    chain[slots + slot, plane] = wins[chunk][slot, first + plane] + chain[tbl[9, slot], plane]
+                return unused
+
+            lax.fori_loop(0, slots, link_fixed, 0)
+            lax.fori_loop(0, slots, link_moved, 0)
+
+            def pack(i, unused, chain=chain, chunk=chunk):
+                outs1[chunk][0, i] = chain[last[across * norb + i]]
+                outs1[chunk][0, part + i] = chain[last[corner * norb + i]]
+                outs1[chunk][1, i] = chain[last[along * norb + part + i]]
+                outs1[chunk][1, part + i] = chain[last[corner * norb + part + i]]
+                return unused
+
+            lax.fori_loop(0, part, pack, 0)
+            swap(chunk, 0).start()
+            swap(chunk, 1).start()
+        chunk = step - 3
+        if 0 <= chunk < count:
+            chain = chains[chunk]
+            swap(chunk, 0).wait_recv()
+
+            def add_across(i, unused, chain=chain, chunk=chunk):
+                outs2[chunk][0, i] = ins1[chunk][0, part + i] + chain[last[along * norb + i]]
+                return unused
+
+            lax.fori_loop(0, part, add_across, 0)
+            swap(chunk, 2).start()
+            swap(chunk, 1).wait_recv()
+
+            def add_along(i, unused, chain=chain, chunk=chunk):
+                outs2[chunk][1, i] = ins1[chunk][1, part + i] + chain[last[across * norb + part + i]]
+                return unused
+
+            lax.fori_loop(0, part, add_along, 0)
+            swap(chunk, 3).start()
+        chunk = step - 4
+        if 0 <= chunk < count:
+            chain = chains[chunk]
+            swap(chunk, 2).wait_recv()
+            swap(chunk, 3).wait_recv()
+            for side in range(2):
+                def keep(i, unused, side=side, chain=chain, chunk=chunk):
+                    orbit = side * part + i
+                    found = ins1[chunk][side, i] + ins2[chunk][side, i]
+                    out[orbit, :, pl.ds(chunk * SUB, SUB)] = found + chain[last[grp * norb + orbit]]
+                    return unused
+
+                lax.fori_loop(0, part, keep, 0)
+    for chunk in range(count):
+        for kind in range(4):
+            swap(chunk, kind).wait_send()
+    relay.drain()
+
+
+def hand_back(table, last, going, staying, norb, chips):
+    chunks, slots, planes, sub, lanes = going.shape
+    vmem = pl.BlockSpec(memory_space=pltpu.VMEM)
+    smem = pl.BlockSpec(memory_space=pltpu.SMEM)
+    dma = pltpu.SemaphoreType.DMA
+    def room(*lead):
+        return [pltpu.VMEM(lead + (planes, sub, lanes), jnp.float32)] * chunks
+    wins = [pltpu.VMEM((slots, 6 * planes, sub, lanes), jnp.float32)] * chunks
+    return pl.pallas_call(
+        functools.partial(hand_back_kernel, chips),
+        in_specs=[smem, smem, vmem, vmem],
+        out_specs=vmem,
+        out_shape=jax.ShapeDtypeStruct((norb, planes, chunks * sub, lanes), jnp.float32),
+        scratch_shapes=wins + room(2 * slots + 1) + room(2, norb) + room(2, norb // 2)
+        + room(2, norb) + room(2, norb // 2)
+        + [dma((chunks, 4)), dma((chunks, 4)), dma((chunks, 2, 5)), dma((chunks, 2, 5))],
+        compiler_params=pltpu.CompilerParams(
+            collective_id=2, has_side_effects=True, vmem_limit_bytes=56 * 1024 * 1024
+        ),
+        name="hand_back",
+    )(table, last, going, staying)
+
+
+def slab_body(orbitals, anchors, pair_slots):
+    groups, places = lax.axis_size("grp"), lax.axis_size("grid")
+    norb_local, cells = orbitals.shape
+    planes = cells // (B * B)
+    each = PAIR_DEV * places
+    assignment = deal_evenly(pair_slots, groups, each)
+    pairs = assignment[lax.axis_index("grp")]
+    offsets = anchors[pairs[:, 1]] - anchors[pairs[:, 0]]
+    dx, dy, dz = offsets[:, 0], offsets[:, 1], offsets[:, 2]
+    slot = lax.broadcasted_iota(jnp.int32, (each,), 0)
+    rising = slot < each // 2
+    second = jnp.where(rising, dx >= 0, dx <= 0)
+    shift = jnp.where(second, dx, -dx)
+    moved_id = jnp.where(second, pairs[:, 1], pairs[:, 0])
+    fixed_id = jnp.where(second, pairs[:, 0], pairs[:, 1])
+    terms = jnp.concatenate([fixed_id, moved_id])
+    at = lax.broadcasted_iota(jnp.int32, (2 * each, 2 * each), 0)
+    before = lax.broadcasted_iota(jnp.int32, (2 * each, 2 * each), 1)
+    found = jnp.where((terms[:, None] == terms[None, :]) & (before < at), before, -1)
+    prior = jnp.max(found, axis=1)
+    prior = jnp.where(prior < 0, 2 * each, prior)
+    norb = anchors.shape[0]
+    orbit = lax.broadcasted_iota(jnp.int32, (norb, 2 * each), 0)
+    index = lax.broadcasted_iota(jnp.int32, (norb, 2 * each), 1)
+    last = jnp.max(jnp.where(terms[None, :] == orbit, index, -1), axis=1)
+    last = jnp.where(last < 0, 2 * each, last)
+    table = jnp.stack([
+        moved_id, fixed_id,
+        jnp.where(rising, 4 * planes, 0) - shift,
+        second.astype(jnp.int32), dy, dz,
+        jnp.where(second, 0, shift),
+        jnp.where(rising, 0, 4 * planes) + shift,
+        prior[:each], prior[each:],
+    ])
+    stacked = orbitals.reshape(norb_local, planes, ROWS, LANES)
+    moved, fixed = bring(table, stacked, each, groups, places // 2)
+    dens, partner = pair_up(table, moved, fixed)
+    pot = solve_slabs(table, dens, places)
+    going, staying = make_terms(table, pot, partner, moved, fixed)
+    out = hand_back(table, last, going, staying, norb_local, places // 2)
+    return out.reshape(norb_local, cells)
+
+
+def slabs_fit(mesh):
+    groups, places = mesh.shape["grp"], mesh.shape["grid"]
+    return groups == 4 and places % 2 == 0 and 4 * (B // places) >= PAD
+
+
 def solution(mesh):
     return jax.shard_map(
-        body,
+        slab_body if slabs_fit(mesh) else owner_body,
         mesh=mesh,
         in_specs=(P("grp", "grid"), P(), P()),
         out_specs=P("grp", "grid"),

time: 388 us -> 274 us (0.71)
  Pallas kernels: 42 us -> 255 us
  blocking collectives: 152 us -> 0 us
  waiting for transfers between devices: 152 us -> 0 us
  between operations: 13.3 us -> 0.12 us
  starting transfers between devices: 11.5 us -> 0 us
    pallas_call x6 -> x5, Pallas kernels: 42 us -> 255 us  [the longest x1 106 us: hand_back(): pl.pallas_call(functools.partial(hand_back_kernel, chips), in_specs=[smem...]
    all_to_all x5 -> x0, blocking collectives: 152 us -> none  [the longest x3 90.1 us: body(): lax.all_to_all(t, 'grid', split_axis=0, concat_axis=0, tiled=True)]
    all_gather x2 -> x0, waiting for transfers between devices: 67.5 us -> none  [body(): lax.all_gather(stacked[:, chunk * rows:(chunk + 1) * rows], 'grp', axis=0...]
    reduce_scatter x2 -> x0, waiting for transfers between devices: 50.7 us -> none  [body(): lax.psum_scatter(summed, 'grp', scatter_dimension=0, tiled=True)]
    all_to_all x3 -> x0, waiting for transfers between devices: 32.7 us -> none  [the longest x2 17.8 us: body(): lax.all_to_all(outgoing[slot], 'grid', split_axis=0, concat_axis=0, tiled...]
    all_to_all x3 -> x0, starting transfers between devices: 11.4 us -> none  [the longest x2 7.11 us: body(): lax.all_to_all(outgoing[slot], 'grid', split_axis=0, concat_axis=0, tiled...]
    unnamed x18, local copies, waits for them, and re-layouts: 10 us -> 14.8 us
  transfers between devices with their start and end apart: 7 -> 0, of which waited for: 6 -> 0; matrix products, arithmetic and copies ran while one was open for 1% -> 0% of each run, Pallas kernels for 9% -> 0%
where the time goes in v1:
time: 274 us; the launch traced here: 273 us
  Pallas kernels  255 us (93%)
  local copies, waits for them, and re-layouts  16.5 us (6%)
    pallas_call x1, Pallas kernels, hand_back(): pl.pallas_call(functools.partial(hand_back_kernel, chips), in_specs=[smem...  106 us
    pallas_call x1, Pallas kernels, bring(): pl.pallas_call(functools.partial(bring_kernel, chips), in_specs=[pl.Block...  99.6 us
    pallas_call x1, Pallas kernels, solve_slabs(): pl.pallas_call(functools.partial(solve_slabs_kernel, places), in_specs=[p...  24.1 us
    unnamed x18, local copies, waits for them, and re-layouts  14.8 us
    pallas_call x1, Pallas kernels, make_terms(): pl.pallas_call(term_kernel, grid_spec=pltpu.PrefetchScalarGridSpec(num_sc...  12.6 us
    pallas_call x1, Pallas kernels, pair_up(): pl.pallas_call(pair_kernel, grid_spec=pltpu.PrefetchScalarGridSpec(num_sc...  12.1 us

profile of v1, /device:TPU:0, one launch (start us, length us, event | category | flops | bytes accessed | tf_op | source)
XLA Modules:
  0.0 273.2 jit_solution(16416704171115261898)
XLA Ops:
  0.0 0.1 add.32
  0.1 0.8 copy.17
  0.9 0.8 copy.14
  1.7 0.1 compare_reduce_fusion
  1.9 0.2 reduce-window.8
  2.0 0.1 subtract_reduce_fusion
  2.1 0.1 compare_and_fusion
  2.2 0.1 select_reduce_fusion
  2.3 0.1 reshape.264
  2.5 0.1 copy.21
  2.5 0.1 fusion.3
  2.7 0.6 gather_fusion.1
  3.2 0.1 copy.20
  3.3 0.1 fusion.2
  3.4 0.6 gather_fusion
  4.0 0.1 compare_reduce_fusion.1
  4.1 0.2 slice_reduce_fusion
  4.4 0.1 pad_add_fusion
  4.4 0.2 select_reduce_fusion.2
  4.6 0.1 select_reduce_fusion.1
  4.7 0.5 compare_select_fusion.2.last
  5.4 3.3 %copy.24 = f32[2,8,256,128]{3,2,1,0:T(8,128)} copy(f32[2,8,256,128]{3,1,2,0:T(8,128)} %bitcast.55) | data formatting | bytes 4194304
  8.7 99.6 %bring.1 = (f32[4,16,8,8,128]{4,3,2,1,0:T(8,128)S(1)}, f32[4,16,8,8,128]{4,3,2,1,0:T(8,128)S(1)}) custom-call(s32[10,16]{1,0:T(8,128)S(1)} %stack.8.tbl, f32[16,8,32,128]{3,2,1,0:T(8,128)} %bitcast.54), custom_call_target="tpu_custom_call" | custom-call | tf_op jit(solution)/shard_map/bring/pallas_call | solution.py:538
  108.3 1.3 copy-done
  109.6 1.3 copy-done.1
  110.9 12.1 %pair_up.1 = (f32[16,8,32,128]{3,2,1,0:T(8,128)}, f32[16,8,32,128]{3,2,1,0:T(8,128)}) custom-call(s32[10,16]{1,0:T(8,128)} %copy-done.4, f32[4,16,8,8,128]{4,3,2,1,0:T(8,128)} %copy-done, f32[4,16,8,8,128]{4,3,2,1,0:T(8,128)} %copy-done.1), custom_call_target="tpu_custom_call" | custom-call | tf_op jit(solution)/shard_map/pair_up/pallas_call | solution.py:571
  123.0 1.6 copy-done.3
  124.6 24.1 %solve_slabs.1.pot = f32[16,8,32,128]{3,2,1,0:T(8,128)S(1)} custom-call(s32[10,16]{1,0:T(8,128)S(1)} %copy-done.5, f32[16,8,32,128]{3,2,1,0:T(8,128)S(1)} %copy-done.3), custom_call_target="tpu_custom_call" | custom-call | tf_op jit(solution)/shard_map/solve_slabs/pallas_call | solution.py:806
  148.7 1.4 copy-done.2
  150.1 12.6 %make_terms.1 = (f32[4,16,8,8,128]{4,3,2,1,0:T(8,128)}, f32[4,16,8,8,128]{4,3,2,1,0:T(8,128)}) custom-call(s32[10,16]{1,0:T(8,128)} %copy-done.4, f32[16,8,32,128]{3,2,1,0:T(8,128)} %copy-done.2, f32[16,8,32,128]{3,2,1,0:T(8,128)} %get-tuple-element.14.partner, f32[4,16,8,8,128]{4,3,2,1,0:T(8,128)} %copy-done, f32[4,16,8,8,128]{4,3,2,1,0:T(8,128)} %copy-done.1), custom_call_target="tpu_custom_call" | custom-call | tf_op jit(solution)/shard_map/make_terms/pallas_call | solution.py:845
  162.7 106.4 %hand_back.1 = f32[16,8,32,128]{3,2,1,0:T(8,128)} custom-call(s32[10,16]{1,0:T(8,128)} %copy-done.4, s32[64]{0:T(128)} %compare_select_fusion.2.last, f32[4,16,8,8,128]{4,3,2,1,0:T(8,128)} %get-tuple-element.15.going, f32[4,16,8,8,128]{4,3,2,1,0:T(8,128)} %get-tuple-element.16.staying), custom_call_target="tpu_custom_call" | custom-call | tf_op jit(solution)/shard_map/hand_back/pallas_call | solution.py:969
  269.1 4.1 %copy.27 = f32[2,8,256,128]{3,1,2,0:T(8,128)} copy(f32[2,8,256,128]{3,2,1,0:T(8,128)} %bitcast.53) | data formatting | bytes 4194304
  (22 shorter events, 0.3 us)
Async XLA Ops:
  5.3 3.3 %copy-start.4 = (s32[10,16]{1,0:T(8,128)}, s32[10,16]{1,0:T(8,128)S(1)}, u32[]{:S(2)}) copy-start(s32[10,16]{1,0:T(8,128)S(1)} %stack.8.tbl) | copy-start | bytes 1924
  108.2 1.3 copy-start
  109.6 1.3 copy-start.1
  110.9 12.1 %copy-start.5 = (s32[10,16]{1,0:T(8,128)S(1)}, s32[10,16]{1,0:T(8,128)}, u32[]{:S(2)}) copy-start(s32[10,16]{1,0:T(8,128)} %copy-done.4) | copy-start | bytes 1924
  123.0 1.6 copy-start.3
  148.7 1.4 copy-start.2

commit v2 on v1

--- a/solution.py
+++ b/solution.py
@@ -311,12 +311,13 @@
     return grp, place, across, along, corner
 
 
-def greet(chips):
-    grp, place, across, along, unused = spot()
+def greet(chips, wide=False):
+    grp, place, across, along, corner = spot()
     chip = place // 2
     core = lax.rem(place, 2)
     barrier = pltpu.get_barrier_semaphore()
-    for device in ((across, place), (along, place), (grp, 2 * chip + 1 - core)):
+    peers = [(across, place), (along, place), (grp, 2 * chip + 1 - core)] + ([(corner, place)] if wide else [])
+    for device in peers:
         pl.semaphore_signal(barrier, inc=1, device_id=device, device_id_type=MESH)
 
     @pl.when(chip > 0)
@@ -328,24 +329,25 @@
         pl.semaphore_signal(barrier, inc=1, device_id=(grp, place + 2), device_id_type=MESH)
 
     ends = jnp.where(chip > 0, 1, 0) + jnp.where(chip < chips - 1, 1, 0)
-    pl.semaphore_wait(barrier, 3 + ends)
+    pl.semaphore_wait(barrier, len(peers) + ends)
 
 
 class Relay:
-    def __init__(self, wins, send_sem, recv_sem, signs, chips):
+    def __init__(self, wins, send_sem, recv_sem, signs, chips, far, mid):
         self.wins, self.send_sem, self.recv_sem, self.signs, self.chips = wins, send_sem, recv_sem, signs, chips
         self.grp, self.place = lax.axis_index("grp"), lax.axis_index("grid")
         self.chip = self.place // 2
         self.core = lax.rem(self.place, 2)
         self.half = wins[0].shape[0] // 2
         self.planes = wins[0].shape[1] // 6
+        self.far, self.mid = far, mid
 
     def offset(self, sign, hop):
         return 2 * self.planes * (2 - hop if sign > 0 else hop)
 
-    def region(self, chunk, side, hop, core):
+    def region(self, chunk, side, hop, core, size):
         start = self.offset(self.signs[side], hop) + self.planes * core
-        return self.wins[chunk].at[pl.ds(side * self.half, self.half), pl.ds(start, self.planes)]
+        return self.wins[chunk].at[pl.ds(side * self.half, size), pl.ds(start, self.planes)]
 
     def comes(self, side, hop):
         source = self.chip - self.signs[side] * hop
@@ -357,23 +359,34 @@
             return (self.chip + 1 < self.chips) & (source >= 0)
         return (self.chip - 1 >= 0) & (source < self.chips)
 
-    def onward(self, chunk, side, hop):
-        here = self.region(chunk, side, hop - 1, self.core)
-        there = self.region(chunk, side, hop, self.core)
+    def spans(self, side, hop, core, act):
+        if hop == 0:
+            act(self.half)
+        elif hop == 2:
+            act(self.far)
+        elif self.mid == self.half:
+            act(self.half)
+        else:
+            near = 1 if self.signs[side] > 0 else 0
+
+            @pl.when(core == near)
+            def whole():
+                act(self.half)
+
+            @pl.when(core != near)
+            def some():
+                act(self.mid)
+
+    def onward(self, chunk, side, hop, size, here=None):
+        source = self.region(chunk, side, hop - 1 if here is None else here, self.core, size)
+        there = self.region(chunk, side, hop, self.core, size)
         return remote(
-            here, there, self.send_sem.at[chunk, side, hop - 1], self.recv_sem.at[chunk, side, hop - 1],
+            source, there, self.send_sem.at[chunk, side, hop - 1], self.recv_sem.at[chunk, side, hop - 1],
             (self.grp, self.place + 2 * self.signs[side]),
         )
 
-    def arriving(self, chunk, side, hop):
-        there = self.region(chunk, side, hop, self.core)
-        return remote(
-            there, there, self.send_sem.at[chunk, side, hop - 1], self.recv_sem.at[chunk, side, hop - 1],
-            (self.grp, self.place + 2 * self.signs[side]),
-        )
-
-    def beside(self, chunk, side, hop, core):
-        part = self.region(chunk, side, hop, core)
+    def beside(self, chunk, side, hop, core, size):
+        part = self.region(chunk, side, hop, core, size)
         return remote(
             part, part, self.send_sem.at[chunk, side, 2 + hop], self.recv_sem.at[chunk, side, 2 + hop],
             (self.grp, 2 * self.chip + 1 - self.core),
@@ -395,52 +408,65 @@
 
                         lax.fori_loop(side * self.half, (side + 1) * self.half, zero, 0)
 
+    def pass_on(self, chunk, side, hop):
+        @pl.when(self.goes(side, hop))
+        def go():
+            self.spans(side, hop, self.core, lambda size: self.onward(chunk, side, hop, size).start())
+
     def begin(self, chunk):
         for side in range(2):
-            self.beside(chunk, side, 0, self.core).start()
-
-            @pl.when(self.goes(side, 1))
-            def go(side=side):
-                self.onward(chunk, side, 1).start()
+            self.pass_on(chunk, side, 1)
+            self.beside(chunk, side, 0, self.core, self.half).start()
+
+    def take(self, chunk, side, hop):
+        @pl.when(self.comes(side, hop))
+        def got():
+            def act(size):
+                self.onward(chunk, side, hop, size, hop).wait_recv()
+
+            self.spans(side, hop, self.core, act)
+
+        if hop < 2:
+            self.pass_on(chunk, side, hop + 1)
+
+        @pl.when(self.comes(side, hop))
+        def share():
+            self.spans(side, hop, self.core, lambda size: self.beside(chunk, side, hop, self.core, size).start())
 
     def first(self, chunk):
         for side in range(2):
-            @pl.when(self.comes(side, 1))
-            def got(side=side):
-                self.arriving(chunk, side, 1).wait_recv()
-                self.beside(chunk, side, 1, self.core).start()
-
-            @pl.when(self.goes(side, 2))
-            def go(side=side):
-                self.onward(chunk, side, 2).start()
+            self.take(chunk, side, 1)
 
     def second(self, chunk):
         for side in range(2):
-            @pl.when(self.comes(side, 2))
-            def got(side=side):
-                self.arriving(chunk, side, 2).wait_recv()
-                self.beside(chunk, side, 2, self.core).start()
+            self.take(chunk, side, 2)
 
     def settle(self, chunk):
+        other = 1 - self.core
         for side in range(2):
-            self.beside(chunk, side, 0, 1 - self.core).wait_recv()
+            self.beside(chunk, side, 0, other, self.half).wait_recv()
             for hop in (1, 2):
                 @pl.when(self.comes(side, hop))
                 def got(side=side, hop=hop):
-                    self.beside(chunk, side, hop, 1 - self.core).wait_recv()
+                    self.spans(side, hop, other, lambda size: self.beside(chunk, side, hop, other, size).wait_recv())
 
     def drain(self):
         for chunk in range(len(self.wins)):
             for side in range(2):
-                self.beside(chunk, side, 0, self.core).wait_send()
+                self.beside(chunk, side, 0, self.core, self.half).wait_send()
                 for hop in (1, 2):
                     @pl.when(self.comes(side, hop))
                     def sent(chunk=chunk, side=side, hop=hop):
-                        self.beside(chunk, side, hop, self.core).wait_send()
+                        self.spans(
+                            side, hop, self.core,
+                            lambda size: self.beside(chunk, side, hop, self.core, size).wait_send(),
+                        )
 
                     @pl.when(self.goes(side, hop))
                     def passed(chunk=chunk, side=side, hop=hop):
-                        self.onward(chunk, side, hop).wait_send()
+                        self.spans(
+                            side, hop, self.core, lambda size: self.onward(chunk, side, hop, size).wait_send()
+                        )
 
 
 def bring_kernel(chips, tbl, orb, moved, fixed, *scratch):
@@ -452,7 +478,7 @@
     norb, planes = orb.shape[:2]
     part = norb // 2
     slots = moved.shape[1]
-    relay = Relay(wins, z_send, z_recv, (1, -1), chips)
+    relay = Relay(wins, z_send, z_recv, (1, -1), chips, slots // 2, slots // 2)
 
     def block(chunk, owner, start, size):
         return pools[chunk].at[pl.ds(owner * norb + start, size)]
@@ -551,29 +577,30 @@
 
 
 def pair_kernel(tbl, moved, fixed, dens, partner):
-    slot = pl.program_id(0)
-    second = tbl[3, slot] > 0
-    dy, dz = tbl[4, slot], tbl[5, slot]
-
-    for x in range(moved.shape[2]):
-        left = moved[:, 0, x].reshape(ROWS, LANES)
-        right = fixed[:, 0, x].reshape(ROWS, LANES)
-        other = shift_plane(jnp.where(second, left, right), dy, dz)
-        dens[0, x] = jnp.where(second, right, left) * other
-        partner[0, x] = other
+    def go(slot, unused):
+        second = tbl[3, slot] > 0
+        dy, dz = tbl[4, slot], tbl[5, slot]
+        for x in range(moved.shape[2]):
+            left = moved[:, slot, x].reshape(ROWS, LANES)
+            right = fixed[:, slot, x].reshape(ROWS, LANES)
+            other = shift_plane(jnp.where(second, left, right), dy, dz)
+            dens[slot, x] = jnp.where(second, right, left) * other
+            partner[slot, x] = other
+        return unused
+
+    lax.fori_loop(0, moved.shape[1], go, 0)
 
 
 def pair_up(table, moved, fixed):
     chunks, slots, planes, sub, lanes = moved.shape
-    tiled = pl.BlockSpec((chunks, 1, planes, sub, lanes), lambda i, t: (0, i, 0, 0, 0))
-    plain = pl.BlockSpec((1, planes, ROWS, lanes), lambda i, t: (i, 0, 0, 0))
+    vmem = pl.BlockSpec(memory_space=pltpu.VMEM)
     shape = jax.ShapeDtypeStruct((slots, planes, ROWS, lanes), jnp.float32)
     return pl.pallas_call(
         pair_kernel,
-        grid_spec=pltpu.PrefetchScalarGridSpec(
-            num_scalar_prefetch=1, grid=(slots,), in_specs=[tiled, tiled], out_specs=[plain, plain]
-        ),
+        in_specs=[pl.BlockSpec(memory_space=pltpu.SMEM), vmem, vmem],
+        out_specs=[vmem, vmem],
         out_shape=[shape, shape],
+        compiler_params=pltpu.CompilerParams(vmem_limit_bytes=24 * 1024 * 1024),
         name="pair_up",
     )(table, moved, fixed)
 
@@ -798,7 +825,7 @@
         tell(step).wait_send()
 
 
-def solve_slabs(table, dens, places):
+def solve_slabs(table, dens, places, ident):
     slots, planes, rows, lanes = dens.shape
     vmem = pl.BlockSpec(memory_space=pltpu.VMEM)
     dma = pltpu.SemaphoreType.DMA
@@ -816,38 +843,40 @@
             dma((WAVES, 2)), dma((WAVES, 2)), dma((places - 1,)), dma((places - 1,)),
         ],
         compiler_params=pltpu.CompilerParams(
-            collective_id=1, has_side_effects=True, vmem_limit_bytes=40 * 1024 * 1024
+            collective_id=ident, has_side_effects=True, vmem_limit_bytes=40 * 1024 * 1024
         ),
         name="solve_slabs",
     )(table, dens)
 
 
 def term_kernel(tbl, pot, partner, moved, fixed, going, staying):
-    slot = pl.program_id(0)
-    second = tbl[3, slot] > 0
-    dy, dz = tbl[4, slot], tbl[5, slot]
     chunks = going.shape[0]
-    for x in range(pot.shape[1]):
-        found = pot[0, x]
-        left = moved[:, 0, x].reshape(ROWS, LANES)
-        right = fixed[:, 0, x].reshape(ROWS, LANES)
-        term_a = found * partner[0, x]
-        term_b = shift_plane(found * jnp.where(second, right, left), -dy, -dz)
-        going[:, 0, x] = jnp.where(second, term_b, term_a).reshape(chunks, SUB, LANES)
-        staying[:, 0, x] = jnp.where(second, term_a, term_b).reshape(chunks, SUB, LANES)
+
+    def go(slot, unused):
+        second = tbl[3, slot] > 0
+        dy, dz = tbl[4, slot], tbl[5, slot]
+        for x in range(pot.shape[1]):
+            found = pot[slot, x]
+            left = moved[:, slot, x].reshape(ROWS, LANES)
+            right = fixed[:, slot, x].reshape(ROWS, LANES)
+            term_a = found * partner[slot, x]
+            term_b = shift_plane(found * jnp.where(second, right, left), -dy, -dz)
+            going[:, slot, x] = jnp.where(second, term_b, term_a).reshape(chunks, SUB, LANES)
+            staying[:, slot, x] = jnp.where(second, term_a, term_b).reshape(chunks, SUB, LANES)
+        return unused
+
+    lax.fori_loop(0, pot.shape[0], go, 0)
 
 
 def make_terms(table, pot, partner, moved, fixed):
-    chunks, slots, planes, sub, lanes = moved.shape
-    tiled = pl.BlockSpec((chunks, 1, planes, sub, lanes), lambda i, t: (0, i, 0, 0, 0))
-    plain = pl.BlockSpec((1, planes, ROWS, lanes), lambda i, t: (i, 0, 0, 0))
+    vmem = pl.BlockSpec(memory_space=pltpu.VMEM)
     shape = jax.ShapeDtypeStruct(moved.shape, jnp.float32)
     return pl.pallas_call(
         term_kernel,
-        grid_spec=pltpu.PrefetchScalarGridSpec(
-            num_scalar_prefetch=1, grid=(slots,), in_specs=[plain, plain, tiled, tiled], out_specs=[tiled, tiled]
-        ),
+        in_specs=[pl.BlockSpec(memory_space=pltpu.SMEM)] + [vmem] * 4,
+        out_specs=[vmem, vmem],
         out_shape=[shape, shape],
+        compiler_params=pltpu.CompilerParams(vmem_limit_bytes=24 * 1024 * 1024),
         name="make_terms",
     )(table, pot, partner, moved, fixed)
 
@@ -860,7 +889,7 @@
     core = lax.rem(place, 2)
     norb, planes = out.shape[:2]
     part = norb // 2
-    relay = Relay(wins, z_send, z_recv, (-1, 1), chips)
+    relay = Relay(wins, z_send, z_recv, (-1, 1), chips, slots // 2, slots // 2)
     greet(chips)
     relay.clear()
 
@@ -981,11 +1010,408 @@
     )(table, last, going, staying)
 
 
-def slab_body(orbitals, anchors, pair_slots):
-    groups, places = lax.axis_size("grp"), lax.axis_size("grid")
-    norb_local, cells = orbitals.shape
-    planes = cells // (B * B)
-    each = PAIR_DEV * places
+def plan_kernel(cap, planes, me_ref, anchors, pairs, tbl, links, fits, spots, lists, tallies, counts):
+    groups = 4
+    orbits = anchors.shape[0] // 3
+    local = orbits // groups
+    entries = pairs.shape[0] // 2
+    each = tbl.shape[1]
+    half = each // 2
+    extra = (groups - 1) * cap
+    final = extra
+    prior = final + local + extra
+    ends = prior + extra
+    worst = 1 << 20
+    me = me_ref[0]
+
+    def reset(o, unused):
+        for h in range(groups):
+            spots[h * orbits + o] = jnp.where(o // local == h, o - h * local, -1)
+        return unused
+
+    lax.fori_loop(0, orbits, reset, 0)
+    for i in range(2 * groups):
+        tallies[i] = 0
+    for i in range(groups * groups):
+        counts[i] = 0
+
+    def clean(i, unused):
+        links[i] = 0
+        links[prior + i] = extra
+        return unused
+
+    lax.fori_loop(0, extra, clean, 0)
+
+    def close(i, unused):
+        links[final + i] = 2 * each
+        return unused
+
+    lax.fori_loop(0, local + extra, close, 0)
+
+    def close_own(i, unused):
+        links[ends + i] = extra
+        return unused
+
+    lax.fori_loop(0, local, close_own, 0)
+
+    def sort(i, tails):
+        a, b = pairs[2 * i], pairs[2 * i + 1]
+        filled = a >= 0
+        reach = jnp.abs(anchors[3 * jnp.maximum(b, 0)] - anchors[3 * jnp.maximum(a, 0)])
+        kind = jnp.where(reach > 2 * planes, 0, jnp.where(reach > planes, 1, 2))
+        tail = jnp.where(kind == 0, tails[0], jnp.where(kind == 1, tails[1], tails[2]))
+
+        @pl.when(filled)
+        def put():
+            lists[kind * entries + tail] = i
+
+        return tuple(tails[k] + jnp.where(filled & (kind == k), 1, 0) for k in range(3))
+
+    zero = jnp.int32(0)
+    tails = lax.fori_loop(0, entries, sort, (zero, zero, zero))
+    fits[0] = 1
+
+    for kind, limit in enumerate((half // 2, 3 * half // 4, half)):
+        def deal(i, unused, kind=kind, limit=limit):
+            entry = lists[kind * entries + i]
+            a, b = pairs[2 * entry], pairs[2 * entry + 1]
+            group_a, group_b = a // local, b // local
+            best, column, side, slot = jnp.int32(worst), zero, zero, zero
+            for h in range(groups):
+                new_a, new_b = spots[h * orbits + a] < 0, spots[h * orbits + b] < 0
+                need_a = jnp.where(new_a, counts[h * groups + jnp.bitwise_xor(group_a, h)] + 1, 0)
+                need_b = jnp.where(new_b, counts[h * groups + jnp.bitwise_xor(group_b, h)] + 1, 0)
+                need_b = need_b + jnp.where(new_a & new_b & (group_a == group_b), 1, 0)
+                need = jnp.maximum(need_a, need_b)
+                up, down = tallies[2 * h], tallies[2 * h + 1]
+                taken = jnp.minimum(up, down)
+                cost = jnp.where(new_a, 2, 0) + jnp.where(new_b, 2, 0) + need + taken
+                score = jnp.where((taken < limit) & (need <= cap), cost, worst)
+                better = score < best
+                best = jnp.where(better, score, best)
+                column = jnp.where(better, h, column)
+                side = jnp.where(better, jnp.where(down < up, 1, 0), side)
+                slot = jnp.where(better, taken, slot)
+
+            @pl.when(best >= worst)
+            def fail():
+                fits[0] = 0
+
+            @pl.when(best < worst)
+            def seat():
+                tallies[2 * column + side] = slot + 1
+                for orbit, group in ((a, group_a), (b, group_b)):
+                    @pl.when(spots[column * orbits + orbit] < 0)
+                    def fetch(orbit=orbit, group=group):
+                        turn = jnp.bitwise_xor(group, column)
+                        taken = counts[column * groups + turn]
+                        spots[column * orbits + orbit] = local + (turn - 1) * cap + taken
+                        counts[column * groups + turn] = taken + 1
+
+                        @pl.when(group == me)
+                        def note():
+                            links[(turn - 1) * cap + taken] = orbit - group * local
+
+                @pl.when(column == me)
+                def fill():
+                    at = side * half + slot
+                    spot_a, spot_b = spots[column * orbits + a], spots[column * orbits + b]
+                    dx = anchors[3 * b] - anchors[3 * a]
+                    rising = side == 0
+                    second = jnp.where(rising, dx, -dx) >= 0
+                    shift = jnp.where(second, dx, -dx)
+                    tbl[0, at] = jnp.where(second, spot_b, spot_a)
+                    tbl[1, at] = jnp.where(second, spot_a, spot_b)
+                    tbl[2, at] = jnp.where(rising, 4 * planes, 0) - shift
+                    tbl[3, at] = jnp.where(second, 1, 0)
+                    tbl[4, at] = anchors[3 * b + 1] - anchors[3 * a + 1]
+                    tbl[5, at] = anchors[3 * b + 2] - anchors[3 * a + 2]
+                    tbl[6, at] = jnp.where(second, 0, shift)
+                    tbl[7, at] = jnp.where(rising, 0, 4 * planes) + shift
+
+            return unused
+
+        lax.fori_loop(0, tails[kind], deal, 0)
+
+    @pl.when(fits[0] > 0)
+    def chain():
+        for row, base in ((1, 0), (0, each)):
+            def link(slot, unused, row=row, base=base):
+                at = final + tbl[row, slot]
+                tbl[9 - row, slot] = links[at]
+                links[at] = base + slot
+                return unused
+
+            lax.fori_loop(0, each, link, 0)
+        for turn in range(1, groups):
+            def hook(i, unused, turn=turn):
+                at = (turn - 1) * cap + i
+                end = ends + links[at]
+                links[prior + at] = links[end]
+                links[end] = at
+                return unused
+
+            lax.fori_loop(0, counts[jnp.bitwise_xor(me, turn) * groups + turn], hook, 0)
+
+
+def make_plan(me, anchors, pair_slots, cap, each, planes):
+    orbits = anchors.shape[0]
+    entries = pair_slots.shape[0] * pair_slots.shape[1]
+    smem = pl.BlockSpec(memory_space=pltpu.SMEM)
+    local = orbits // 4
+    return pl.pallas_call(
+        functools.partial(plan_kernel, cap, planes),
+        in_specs=[smem] * 3,
+        out_specs=[smem] * 3,
+        out_shape=[
+            jax.ShapeDtypeStruct((10, each), jnp.int32),
+            jax.ShapeDtypeStruct((9 * cap + 2 * local,), jnp.int32),
+            jax.ShapeDtypeStruct((1,), jnp.int32),
+        ],
+        scratch_shapes=[
+            pltpu.SMEM((4 * orbits,), jnp.int32), pltpu.SMEM((3 * entries,), jnp.int32),
+            pltpu.SMEM((8,), jnp.int32), pltpu.SMEM((16,), jnp.int32),
+        ],
+        name="plan",
+    )(me, anchors.reshape(-1), pair_slots.reshape(-1))
+
+
+def fetch_kernel(chips, cap, tbl, links, orb, moved, fixed, *scratch):
+    count = moved.shape[0]
+    owns, parcels, pools, wins = [scratch[i * count : (i + 1) * count] for i in range(4)]
+    own_sem, xy_send, xy_recv, z_send, z_recv = scratch[4 * count :]
+    grp, place, across, along, corner = spot()
+    core = lax.rem(place, 2)
+    norb, planes = orb.shape[:2]
+    slots = moved.shape[1]
+    half = slots // 2
+    relay = Relay(wins, z_send, z_recv, (1, -1), chips, half // 2, 3 * half // 4)
+
+    def stage(chunk, kind):
+        dst = owns[chunk] if kind == 0 else pools[chunk].at[pl.ds(0, norb)]
+        return pltpu.make_async_copy(orb.at[:, :, pl.ds(chunk * SUB, SUB)], dst, own_sem.at[chunk, kind])
+
+    def parcel(chunk, kind):
+        return remote(
+            parcels[chunk].at[pl.ds(kind * cap, cap)], pools[chunk].at[pl.ds(norb + kind * cap, cap)],
+            xy_send.at[chunk, kind], xy_recv.at[chunk, kind], ((across, along, corner)[kind], place),
+        )
+
+    for chunk in range(count):
+        stage(chunk, 0).start()
+    for chunk in range(count):
+        stage(chunk, 1).start()
+    greet(chips, True)
+
+    def pack(chunk):
+        stage(chunk, 0).wait()
+
+        def put(i, unused):
+            parcels[chunk][i] = owns[chunk][links[i]]
+            return unused
+
+        lax.fori_loop(0, 3 * cap, put, 0)
+
+    def send(chunk):
+        for kind in (2, 0, 1):
+            parcel(chunk, kind).start()
+
+    pack(0)
+    for chunk in range(1, count):
+        pack(chunk)
+        send(chunk - 1)
+    send(count - 1)
+    relay.clear()
+    for step in range(count + 3):
+        chunk = step
+        if chunk < count:
+            stage(chunk, 1).wait()
+            for kind in range(3):
+                parcel(chunk, kind).wait_recv()
+            for side in range(2):
+                start = relay.offset(relay.signs[side], 0) + planes * core
+
+                def pick(slot, unused, start=start, chunk=chunk):
+                    wins[chunk][slot, pl.ds(start, planes)] = pools[chunk][tbl[0, slot]]
+                    return unused
+
+                lax.fori_loop(side * half, (side + 1) * half, pick, 0)
+
+            def hold(slot, unused, chunk=chunk):
+                fixed[chunk, slot] = pools[chunk][tbl[1, slot]]
+                return unused
+
+            lax.fori_loop(0, slots, hold, 0)
+            relay.begin(chunk)
+        chunk = step - 1
+        if 0 <= chunk < count:
+            relay.first(chunk)
+        chunk = step - 2
+        if 0 <= chunk < count:
+            relay.second(chunk)
+        chunk = step - 3
+        if 0 <= chunk < count:
+            relay.settle(chunk)
+
+            def choose(slot, unused, chunk=chunk):
+                first = tbl[2, slot] + planes * core
+                for plane in range(planes):
+                    moved[chunk, slot, plane] = wins[chunk][slot, first + plane]
+                return unused
+
+            lax.fori_loop(0, slots, choose, 0)
+    for chunk in range(count):
+        for kind in range(3):
+            parcel(chunk, kind).wait_send()
+    relay.drain()
+
+
+def fetch(table, links, stacked, slots, chips, cap):
+    norb, planes, rows, lanes = stacked.shape
+    chunks = rows // SUB
+    vmem = pl.BlockSpec(memory_space=pltpu.VMEM)
+    smem = pl.BlockSpec(memory_space=pltpu.SMEM)
+    dma = pltpu.SemaphoreType.DMA
+    shape = jax.ShapeDtypeStruct((chunks, slots, planes, SUB, lanes), jnp.float32)
+
+    def room(count, deep=planes):
+        return [pltpu.VMEM((count, deep, SUB, lanes), jnp.float32)] * chunks
+
+    return pl.pallas_call(
+        functools.partial(fetch_kernel, chips, cap),
+        in_specs=[smem, smem, pl.BlockSpec(memory_space=pl.ANY)],
+        out_specs=[vmem, vmem],
+        out_shape=[shape, shape],
+        scratch_shapes=room(norb) + room(3 * cap) + room(norb + 3 * cap) + room(slots, 6 * planes)
+        + [dma((chunks, 2)), dma((chunks, 3)), dma((chunks, 3)), dma((chunks, 2, 5)), dma((chunks, 2, 5))],
+        compiler_params=pltpu.CompilerParams(
+            collective_id=3, has_side_effects=True, vmem_limit_bytes=48 * 1024 * 1024
+        ),
+        name="fetch",
+    )(table, links, stacked)
+
+
+def give_kernel(chips, cap, tbl, links, going, staying, out, *scratch):
+    count, slots = going.shape[:2]
+    wins, chains, parcels, backs, tallied = [scratch[i * count : (i + 1) * count] for i in range(5)]
+    xy_send, xy_recv, z_send, z_recv = scratch[5 * count :]
+    grp, place, across, along, corner = spot()
+    core = lax.rem(place, 2)
+    norb, planes = out.shape[:2]
+    half = slots // 2
+    extra = 3 * cap
+    final = extra
+    prior = final + norb + extra
+    ends = prior + extra
+    relay = Relay(wins, z_send, z_recv, (-1, 1), chips, half // 2, 3 * half // 4)
+    greet(chips, True)
+
+    def load(chunk):
+        for side in range(2):
+            at = relay.offset(relay.signs[side], 0) + planes * core
+
+            def place_in(slot, unused, at=at):
+                wins[chunk][slot, pl.ds(at, planes)] = going[chunk, slot]
+                return unused
+
+            lax.fori_loop(side * half, (side + 1) * half, place_in, 0)
+
+    def parcel(chunk, kind):
+        return remote(
+            parcels[chunk].at[pl.ds(kind * cap, cap)], backs[chunk].at[pl.ds(kind * cap, cap)],
+            xy_send.at[chunk, kind], xy_recv.at[chunk, kind], ((across, along, corner)[kind], place),
+        )
+
+    load(0)
+    load(1)
+    relay.begin(0)
+    for chunk in range(2, count):
+        load(chunk)
+    relay.begin(1)
+    relay.clear()
+    for step in range(count + 3):
+        if step < count:
+            relay.first(step)
+            if step + 2 < count:
+                relay.begin(step + 2)
+        chunk = step - 1
+        if 0 <= chunk < count:
+            relay.second(chunk)
+        chunk = step - 2
+        if 0 <= chunk < count:
+            relay.settle(chunk)
+            chain = chains[chunk]
+            chain[2 * slots] = jnp.zeros(chain.shape[1:], jnp.float32)
+
+            def link_fixed(slot, unused, chain=chain, chunk=chunk):
+                chain[slot] = staying[chunk, slot] + chain[tbl[8, slot]]
+                return unused
+
+            def link_moved(slot, unused, chain=chain, chunk=chunk):
+                first = tbl[7, slot] + planes * core
+                for plane in range(planes):
+                    chain[slots + slot, plane] = wins[chunk][slot, first + plane] + chain[tbl[9, slot], plane]
+                return unused
+
+            lax.fori_loop(0, slots, link_fixed, 0)
+            lax.fori_loop(0, slots, link_moved, 0)
+
+            def pack(i, unused, chain=chain, chunk=chunk):
+                parcels[chunk][i] = chain[links[final + norb + i]]
+                return unused
+
+            lax.fori_loop(0, extra, pack, 0)
+            for kind in (2, 0, 1):
+                parcel(chunk, kind).start()
+        chunk = step - 3
+        if 0 <= chunk < count:
+            total_of = tallied[chunk]
+            total_of[extra] = jnp.zeros(total_of.shape[1:], jnp.float32)
+            for kind in range(3):
+                parcel(chunk, kind).wait_recv()
+
+            def gather(i, unused, total_of=total_of, chunk=chunk):
+                total_of[i] = backs[chunk][i] + total_of[links[prior + i]]
+                return unused
+
+            lax.fori_loop(0, extra, gather, 0)
+
+            def keep(orbit, unused, total_of=total_of, chunk=chunk):
+                found = total_of[links[ends + orbit]] + chains[chunk][links[final + orbit]]
+                out[orbit, :, pl.ds(chunk * SUB, SUB)] = found
+                return unused
+
+            lax.fori_loop(0, norb, keep, 0)
+    for chunk in range(count):
+        for kind in range(3):
+            parcel(chunk, kind).wait_send()
+    relay.drain()
+
+
+def give(table, links, going, staying, norb, chips, cap):
+    chunks, slots, planes, sub, lanes = going.shape
+    vmem = pl.BlockSpec(memory_space=pltpu.VMEM)
+    smem = pl.BlockSpec(memory_space=pltpu.SMEM)
+    dma = pltpu.SemaphoreType.DMA
+
+    def room(count, deep=planes):
+        return [pltpu.VMEM((count, deep, sub, lanes), jnp.float32)] * chunks
+
+    return pl.pallas_call(
+        functools.partial(give_kernel, chips, cap),
+        in_specs=[smem, smem, vmem, vmem],
+        out_specs=vmem,
+        out_shape=jax.ShapeDtypeStruct((norb, planes, chunks * sub, lanes), jnp.float32),
+        scratch_shapes=room(slots, 6 * planes) + room(2 * slots + 1) + room(3 * cap) + room(3 * cap)
+        + room(3 * cap + 1) + [dma((chunks, 3)), dma((chunks, 3)), dma((chunks, 2, 5)), dma((chunks, 2, 5))],
+        compiler_params=pltpu.CompilerParams(
+            collective_id=4, has_side_effects=True, vmem_limit_bytes=48 * 1024 * 1024
+        ),
+        name="give",
+    )(table, links, going, staying)
+
+
+def full_tables(anchors, pair_slots, planes, groups, each):
     assignment = deal_evenly(pair_slots, groups, each)
     pairs = assignment[lax.axis_index("grp")]
     offsets = anchors[pairs[:, 1]] - anchors[pairs[:, 0]]
@@ -1015,12 +1441,36 @@
         jnp.where(rising, 0, 4 * planes) + shift,
         prior[:each], prior[each:],
     ])
+    return table, last
+
+
+def slab_body(orbitals, anchors, pair_slots):
+    groups, places = lax.axis_size("grp"), lax.axis_size("grid")
+    norb_local, cells = orbitals.shape
+    planes = cells // (B * B)
+    each = PAIR_DEV * places
+    chips = places // 2
+    cap = 7 * norb_local // 16
+    me = jnp.full((1,), lax.axis_index("grp"), jnp.int32)
+    plan, links, fits = make_plan(me, anchors, pair_slots, cap, each, planes)
     stacked = orbitals.reshape(norb_local, planes, ROWS, LANES)
-    moved, fixed = bring(table, stacked, each, groups, places // 2)
-    dens, partner = pair_up(table, moved, fixed)
-    pot = solve_slabs(table, dens, places)
-    going, staying = make_terms(table, pot, partner, moved, fixed)
-    out = hand_back(table, last, going, staying, norb_local, places // 2)
+
+    def lean(stacked, anchors, pair_slots, plan, links):
+        moved, fixed = fetch(plan, links, stacked, each, chips, cap)
+        dens, partner = pair_up(plan, moved, fixed)
+        pot = solve_slabs(plan, dens, places, 1)
+        going, staying = make_terms(plan, pot, partner, moved, fixed)
+        return give(plan, links, going, staying, norb_local, chips, cap)
+
+    def full(stacked, anchors, pair_slots, plan, links):
+        table, last = full_tables(anchors, pair_slots, planes, groups, each)
+        moved, fixed = bring(table, stacked, each, groups, chips)
+        dens, partner = pair_up(table, moved, fixed)
+        pot = solve_slabs(table, dens, places, 5)
+        going, staying = make_terms(table, pot, partner, moved, fixed)
+        return hand_back(table, last, going, staying, norb_local, chips)
+
+    out = lax.cond(fits[0] > 0, lean, full, stacked, anchors, pair_slots, plan, links)
     return out.reshape(norb_local, cells)
 
 

time: 274 us -> 183 us (0.67)
  Pallas kernels: 255 us -> 173 us
  local copies, waits for them, and re-layouts: 16.5 us -> 8.87 us
    pallas_call x4 -> x5, Pallas kernels: 231 us -> 149 us  [the longest x1 68.5 us: give(): pl.pallas_call(functools.partial(give_kernel, chips, cap), in_specs=[smem...]
    unnamed x18 -> x9, local copies, waits for them, and re-layouts: 14.8 us -> 4.9 us
where the time goes in v2:
time: 183 us
  Pallas kernels  173 us (95%)
  local copies, waits for them, and re-layouts  8.87 us (5%)
    pallas_call x1, Pallas kernels, give(): pl.pallas_call(functools.partial(give_kernel, chips, cap), in_specs=[smem...  68.5 us
    pallas_call x1, Pallas kernels, fetch(): pl.pallas_call(functools.partial(fetch_kernel, chips, cap), in_specs=[sme...  61.1 us
    pallas_call x1, Pallas kernels, solve_slabs(): pl.pallas_call(functools.partial(solve_slabs_kernel, places), in_specs=[p...  24 us
    pallas_call x1, Pallas kernels, make_plan(): pl.pallas_call(functools.partial(plan_kernel, cap, planes), in_specs=[sme...  14.1 us
    unnamed x9, local copies, waits for them, and re-layouts  4.9 us

profile of v2, /device:TPU:0, one launch (start us, length us, event | category | flops | bytes accessed | tf_op | source)
XLA Modules:
  0.0 183.1 jit_solution(8806727317227473593)
XLA Ops:
  0.0 0.8 copy.19
  0.8 0.7 reshape.279.anchors
  1.5 0.8 copy.20
  2.3 0.7 reshape.280.pairs
  3.0 14.1 %plan.1 = (s32[10,16]{1,0:T(8,128)S(1)}, s32[95]{0:T(128)S(1)}, s32[1]{0:T(128)}) custom-call(s32[1]{0:T(128)} %bitcast.4.me_ref, s32[192]{0:T(256)} %reshape.279.anchors, s32[256]{0:T(256)} %reshape.280.pairs), custom_call_target="tpu_custom_call" | custom-call | tf_op jit(solution)/shard_map/plan/pallas_call | solution.py:1162
  17.7 0.0 copy-start.5
  17.7 0.0 copy-start.6
  17.7 2.0 %copy.29 = f32[2,8,256,128]{3,2,1,0:T(8,128)S(1)} copy(f32[2,8,256,128]{3,1,2,0:T(8,128)} %bitcast.64) | data formatting | bytes 4194304
  19.7 0.0 copy-done.5
  19.7 0.0 copy-done.6
  19.8 162.0 %conditional.1 = (f32[16,32768]{1,0:T(8,128)S(1)}) conditional(s32[]{:T(128)} %bitcast.5, (s32[32,4,2]{0,2,1:T(2,128)S(1)}, s32[64,3]{0,1:T(4,128)S(1)}, f32[16,8,32,128]{3,2,1,0:T(8,128)S(1)}) %tuple.37, (s32[10,16]{1,0:T(8,128)S(1)}, s32[95]{0:T(128)S(1)}, f32[16,8,32,128]{3,2,1,0:T(8,128)S(1)}) %tuple.34), branch_computations={%region_0.5_spmd, %region_5.6_spmd} | conditional | flops 80102 | bytes 21019750 | solution.py:1473
  19.8 61.1 %fetch.1 = (f32[4,16,8,8,128]{4,3,2,1,0:T(8,128)S(1)}, f32[4,16,8,8,128]{4,3,2,1,0:T(8,128)S(1)}) custom-call(s32[10,16]{1,0:T(8,128)S(1)} %get-tuple-element.30.tbl, s32[95]{0:T(128)S(1)} %get-tuple-element.31.links, f32[16,8,32,128]{3,2,1,0:T(8,128)S(1)} %get-tuple-element.32.orb), custom_call_target="tpu_custom_call" | custom-call | tf_op jit(solution)/shard_map/cond/branch_1_fun/fetch/pallas_call | solution.py:1280
  80.9 2.8 %pair_up.3 = (f32[16,8,32,128]{3,2,1,0:T(8,128)S(1)}, f32[16,8,32,128]{3,2,1,0:T(8,128)S(1)}) custom-call(s32[10,16]{1,0:T(8,128)S(1)} %get-tuple-element.30.tbl, f32[4,16,8,8,128]{4,3,2,1,0:T(8,128)S(1)} %get-tuple-element.33.moved, f32[4,16,8,8,128]{4,3,2,1,0:T(8,128)S(1)} %get-tuple-element.34.fixed), custom_call_target="tpu_custom_call" | custom-call | tf_op jit(solution)/shard_map/cond/branch_1_fun/pair_up/pallas_call | solution.py:598
  83.7 24.0 %solve_slabs.3.pot = f32[16,8,32,128]{3,2,1,0:T(8,128)S(1)} custom-call(s32[10,16]{1,0:T(8,128)S(1)} %get-tuple-element.30.tbl, f32[16,8,32,128]{3,2,1,0:T(8,128)S(1)} %get-tuple-element.35.dens), custom_call_target="tpu_custom_call" | custom-call | tf_op jit(solution)/shard_map/cond/branch_1_fun/solve_slabs/pallas_call | solution.py:833
  107.7 2.8 %make_terms.3 = (f32[4,16,8,8,128]{4,3,2,1,0:T(8,128)S(1)}, f32[4,16,8,8,128]{4,3,2,1,0:T(8,128)S(1)}) custom-call(s32[10,16]{1,0:T(8,128)S(1)} %get-tuple-element.30.tbl, f32[16,8,32,128]{3,2,1,0:T(8,128)S(1)} %solve_slabs.3.pot, f32[16,8,32,128]{3,2,1,0:T(8,128)S(1)} %get-tuple-element.36.partner, f32[4,16,8,8,128]{4,3,2,1,0:T(8,128)S(1)} %get-tuple-element.33.moved, ...), custom_call_target="tpu_custom_call" | custom-call | tf_op jit(solution)/shard_map/cond/branch_1_fun/make_terms/pallas_call | solution.py:874
  110.5 0.0 copy-start.2
  110.5 1.3 copy-done.2
  111.9 68.5 %give.1 = f32[16,8,32,128]{3,2,1,0:T(8,128)S(1)} custom-call(s32[10,16]{1,0:T(8,128)S(1)} %get-tuple-element.30.tbl, s32[95]{0:T(128)S(1)} %get-tuple-element.31.links, f32[4,16,8,8,128]{4,3,2,1,0:T(8,128)S(1)} %get-tuple-element.37.going, f32[4,16,8,8,128]{4,3,2,1,0:T(8,128)} %copy-done.2), custom_call_target="tpu_custom_call" | custom-call | tf_op jit(solution)/shard_map/cond/branch_1_fun/give/pallas_call | solution.py:1400
  180.4 1.2 copy.32
  181.8 0.0 copy-start.4
  181.8 1.3 copy-done.4
Async XLA Ops:
  17.7 2.0 %copy-start.5 = (s32[32,4,2]{0,2,1:T(2,128)S(1)}, s32[32,4,2]{0,2,1:T(2,128)}, u32[]{:S(2)}) copy-start(s32[32,4,2]{0,2,1:T(2,128)} %param.7) | copy-start | bytes 3076
  17.7 2.0 %copy-start.6 = (s32[64,3]{0,1:T(4,128)S(1)}, s32[64,3]{0,1:T(4,128)}, u32[]{:S(2)}) copy-start(s32[64,3]{0,1:T(4,128)} %param.6) | copy-start | bytes 2308
  110.5 1.3 copy-start.2
  181.8 1.3 copy-start.4
